TPU v7x, 32 devices: a whole 2x2x4 slice. The times are simulated.
32 devices in a mesh: row: 4 (over x, core), col: 8 (over z, y).
Axes of the slice: x: 2, y: 2, z: 4, core: 2. Of those that a mesh axis runs over, the one named last changes fastest.
Arguments:
- momentum: float32 [5120, 27648], P('row', 'col'), may hold values from -130 to 130, as said below
- activations: bfloat16 [2048, 5120], P(None, 'row'), may hold values from -6 to 6
- out_grads: bfloat16 [2048, 27648], P(None, 'col'), may hold values from -0.125 to 0.125
- basis: float32 [27648, 256], P('col'), may hold values from -6 to 6
Outputs:
- new_momentum: float32 [5120, 27648], P('row', 'col')
- left_basis: float32 [5120, 256], P('row')
- new_basis: float32 [27648, 256], P('col')
Inputs may be any that keep to these rules, and one draw needn't show every extreme that they name: `momentum`: Real-valued entries of order one with varying row and column scales.
All inputs are finite; a program needn't handle non-finite values.
Results may differ from a plain program's by a relative error of at most 0.0003.
Values sent between devices are 32-bit elements; how exact they have to be, the bound alone decides.
No kernel may reach another device: no remote copies, remote signals or barrier semaphores. Data moves between devices by JAX's collectives and lax.ppermute only.
A program may use at most 128 MiB of HBM per device.

v0:
```python
import math

import jax
import jax.numpy as jnp
from jax import lax
from jax.sharding import PartitionSpec as P

D = 5120
F = 27648


EPS = 1e-06
HIGH = lax.Precision.HIGHEST


def left_product(block, factor_rows):
    return lax.dot_general(
        block,
        factor_rows,
        (((0,), (0,)), ((), ())),
        precision=HIGH,
        preferred_element_type=jnp.float32,
    )


def invert_gram(gram_total):
    factor = jnp.linalg.cholesky(gram_total)
    identity = jnp.eye(factor.shape[0], dtype=jnp.float32)
    return jax.scipy.linalg.solve_triangular(factor, identity, lower=True).T


def shards(momentum, activations, out_grads, basis):
    gradient = lax.dot_general(
        activations, out_grads, (((0,), (0,)), ((), ())), preferred_element_type=jnp.float32
    )
    merged = momentum + gradient
    block_rows = lax.psum(jnp.dot(merged, basis, precision=HIGH), "col")
    gram_part = jnp.dot(block_rows.T, block_rows, precision=HIGH)
    gram_total = lax.psum(gram_part, "row")
    inverse_t = invert_gram(gram_total)
    ortho = jnp.dot(block_rows, inverse_t, precision=HIGH)
    coeff_part = left_product(merged, ortho)
    coeffs = lax.psum(coeff_part, "row")
    squares = jnp.sum(coeffs * coeffs, axis=0)
    sq_total = lax.psum(squares, "col")
    new_momentum = merged - 0.5 * jnp.dot(ortho, coeffs.T, precision=HIGH)
    inv_norm = lax.rsqrt(sq_total / F + EPS)
    new_basis = coeffs * inv_norm[None, :]
    left_basis = ortho * jnp.float32(math.sqrt(D))
    return (new_momentum, left_basis, new_basis)


def solution(mesh):
    return jax.shard_map(
        shards,
        mesh=mesh,
        in_specs=(P("row", "col"), P(None, "row"), P(None, "col"), P("col", None)),
        out_specs=(P("row", "col"), P("row", None), P("col", None)),
        check_vma=False,
    )
```

profile of v0, /device:TPU:0, one launch (start us, length us, event | category | flops | bytes accessed | tf_op | source)
XLA Modules:
  0.0 406.0 jit_solution(12141631374180239289)
XLA Ops:
  7.2 29.5 %convolution_add_fusion = f32[1280,3456]{1,0:T(8,128)} fusion(f32[1280,3456]{1,0:T(8,128)} %param.4, bf16[2048,1280]{1,0:T(8,128)(2,1)} %param.5, bf16[2048,3456]{1,0:T(8,128)(2,1)} %param.6), kind=kOutput, calls=%fused_computation.2 | convolution fusion | flops 18123816960 | bytes 54788096 | tf_op jit(solution)/shard_map/dot_general | solution.py:33
  36.7 18.5 %fusion.15 = f32[1280,256]{1,0:T(8,128)} fusion(f32[1280,3456]{1,0:T(8,128)} %convolution_add_fusion, f32[3456,256]{1,0:T(8,128)S(1)} %copy-done), kind=kOutput, calls=%fused_computation.41 | convolution fusion | flops 13589544960 | bytes 22544384 | tf_op jit(solution)/shard_map/dot_general | solution.py:37
  55.2 0.2 all-reduce.7.cloned.1.call-start
  55.4 86.3 %all-reduce.5.cloned.1.call-done = f32[1280,256]{1,0:T(8,128)} async-done(((f32[1280,256]{1,0:T(8,128)}), f32[1280,256]{1,0:T(8,128)}) %all-reduce.5.cloned.1.call-update) | async-done | bytes 1310736 | tf_op jit(solution)/shard_map/psum | solution.py:37
  141.7 4.7 %fusion.16 = f32[256,256]{0,1:T(8,128)} fusion(f32[1280,256]{1,0:T(8,128)} %all-reduce.5.cloned.1.call-done), kind=kOutput, calls=%fused_computation.42 | convolution fusion | flops 1006632960 | bytes 1572864 | tf_op jit(solution)/shard_map/dot_general | solution.py:38
  146.5 0.0 all-reduce.9.cloned.1.call-start
  146.6 31.4 %all-reduce.7.cloned.1.call-done = f32[256,256]{0,1:T(8,128)} async-done(((f32[256,256]{0,1:T(8,128)}), f32[256,256]{0,1:T(8,128)}) %all-reduce.7.cloned.1.call-update) | async-done | bytes 262160 | tf_op jit(solution)/shard_map/psum | solution.py:39
  178.0 1.1 copy.8
  179.0 1.0 fusion.5
  180.0 11.7 %cholesky.50 = f32[128,128]{1,0:T(8,128)S(1)} custom-call(f32[128,128]{1,0:T(8,128)S(1)} %cholesky.118), custom_call_target="Cholesky" | custom-call | tf_op jit(solution)/shard_map/jit(cholesky)/cholesky | solution.py:27
  191.8 9.8 %custom-call.15 = f32[1,128,128]{1,2,0:T(8,128)S(1)} custom-call(f32[1,128,128]{2,1,0:T(8,128)S(1)} %get-tuple-element.24), custom_call_target="InvertDiagBlocksLowerTriangular" | custom-call | tf_op jit(solution)/shard_map/jit(cholesky)/cholesky | solution.py:27
  201.6 0.2 constant_dynamic-update-slice_fusion.1
  201.9 0.3 convolution_subtract_fusion.1
  202.1 11.7 %cholesky.105 = f32[128,128]{1,0:T(8,128)S(1)} custom-call(f32[128,128]{1,0:T(8,128)S(1)} %convolution_subtract_fusion.1), custom_call_target="Cholesky" | custom-call | tf_op jit(solution)/shard_map/jit(cholesky)/cholesky | solution.py:27
  213.9 0.7 compare_reduce_fusion
  215.9 0.1 triangular_solve.63
  215.9 4.2 %while.1 = (s32[]{:T(128)}, f32[256,256]{1,0:T(8,128)S(1)}, s32[2,2]{1,0:T(2,128)S(1)}, f32[2,128,128]{2,1,0:T(8,128)S(1)}, s32[]{:T(128)}) while((s32[]{:T(128)}, f32[256,256]{1,0:T(8,128)S(1)}, s32[2,2]{1,0:T(2,128)S(1)}, f32[2,128,128]{2,1,0:T(8,128)S(1)}, s32[]{:T(128)}) %tuple.28), condition=%wide.while_cond, body=%wide.while_body.sunk | while | flops 2 | bytes 131189 | solution.py:29
  216.2 0.6 fusion.34
  216.7 1.4 bitcast_dynamic-update-slice_fusion.2
  218.1 0.6 fusion.34
  218.7 1.4 bitcast_dynamic-update-slice_fusion.2
  220.1 19.7 %custom-call.16 = f32[2,128,128]{1,2,0:T(8,128)S(1)} custom-call(f32[2,128,128]{2,1,0:T(8,128)S(1)} %get-tuple-element.10), custom_call_target="InvertDiagBlocksLowerTriangular" | custom-call | tf_op jit(solution)/shard_map/jit(_solve_triangular)/triangular_solve | solution.py:29
  239.8 0.3 fusion.6
  240.1 0.3 convolution_subtract_fusion
  240.3 0.3 fusion.9
  240.7 2.3 broadcast_multiply_fusion.1
  242.9 32.2 %fusion.17 = f32[3456,256]{1,0:T(8,128)} fusion(f32[1280,3456]{1,0:T(8,128)} %convolution_add_fusion, f32[1280,256]{1,0:T(8,128)S(1)} %get-tuple-element.28), kind=kOutput, calls=%fused_computation.43 | convolution fusion | flops 13589544960 | bytes 22544384 | tf_op jit(solution)/shard_map/dot_general | solution.py:17
  275.2 75.0 %all-reduce.9.cloned.1.call-done = f32[3456,256]{1,0:T(8,128)} async-done(((f32[3456,256]{1,0:T(8,128)}), f32[3456,256]{1,0:T(8,128)}) %all-reduce.9.cloned.1.call-update) | async-done | bytes 3538960 | tf_op jit(solution)/shard_map/psum | solution.py:43
  350.1 2.5 multiply_reduce_fusion
  352.6 21.6 %psum.31 = f32[256]{0:T(256)S(1)} all-reduce(f32[256]{0:T(256)S(1)} %multiply_reduce_fusion), channel_id=1, replica_groups=mesh['row'=4,'col'=8] {'col'}, use_global_device_ids=true, to_apply=%region_8.9 | all-reduce | flops 256 | bytes 2048 | tf_op jit(solution)/shard_map/psum | solution.py:45
  374.2 22.7 %fusion = f32[1280,3456]{1,0:T(8,128)} fusion(f32[1280,3456]{1,0:T(8,128)} %convolution_add_fusion, f32[1280,256]{1,0:T(8,128)} %copy-done.3, f32[3456,256]{1,0:T(8,128)} %all-reduce.9.cloned.1.call-done), kind=kOutput, calls=%fused_computation.4 | convolution fusion | flops 13598392320 | bytes 40239104 | tf_op jit(solution)/shard_map/dot_general | solution.py:46
  397.0 2.0 broadcast_multiply_fusion
  (25 shorter events, 0.3 us)
Async XLA Ops:
  7.2 29.5 %copy-start = (f32[3456,256]{1,0:T(8,128)S(1)}, f32[3456,256]{1,0:T(8,128)}, u32[]{:S(2)}) copy-start(f32[3456,256]{1,0:T(8,128)} %param.7) | copy-start | bytes 10616836
  7.2 134.5 %all-reduce.5.cloned.1.call-start = ((), (), s32[]{:S(2)}) async-start(), calls=%async_computation | async-start | bytes 2621440 | tf_op jit(solution)/shard_map/psum | solution.py:37
  55.2 122.8 %all-reduce.7.cloned.1.call-start = ((), (), s32[]{:S(2)}) async-start(), calls=%async_computation.1 | async-start | bytes 524288 | tf_op jit(solution)/shard_map/psum | solution.py:39
  141.7 99.0 %copy-start.4 = (f32[1280,256]{1,0:T(8,128)S(1)}, f32[1280,256]{1,0:T(8,128)}, u32[]{:S(2)}) copy-start(f32[1280,256]{1,0:T(8,128)} %all-reduce.5.cloned.1.call-done) | copy-start | bytes 3932164
  146.5 203.7 %all-reduce.9.cloned.1.call-start = ((), (), s32[]{:S(2)}) async-start(), calls=%async_computation.2 | async-start | bytes 7077888 | tf_op jit(solution)/shard_map/psum | solution.py:43
  242.9 32.2 %copy-start.3 = (f32[1280,256]{1,0:T(8,128)}, f32[1280,256]{1,0:T(8,128)S(1)}, u32[]{:S(2)}) copy-start(f32[1280,256]{1,0:T(8,128)S(1)} %get-tuple-element.28) | copy-start | bytes 3932164
  374.2 22.7 %copy-start.2 = (f32[3456,256]{1,0:T(8,128)S(1)}, f32[3456,256]{1,0:T(8,128)}, u32[]{:S(2)}) copy-start(f32[3456,256]{1,0:T(8,128)} %all-reduce.9.cloned.1.call-done) | copy-start | bytes 10616836
  374.2 24.8 %copy-start.1 = (f32[3456,256]{1,0:T(8,128)S(1)}, f32[3456,256]{1,0:T(8,128)}, u32[]{:S(2)}) copy-start(f32[3456,256]{1,0:T(8,128)} %param.7) | copy-start | bytes 10616836
Sparse Core Ops, SparseCore 0:
  55.3 86.3 all-reduce.4
  146.6 31.3 all-reduce.6
  275.3 74.8 all-reduce.8
where the time goes:
time: 414 us; the launch traced here: 406 us
  waiting for transfers between devices  193 us (47%)
  matrix products  111 us (27%)
  other arithmetic  59.2 us (14%)
  blocking collectives  21.6 us (5%)
  between operations  15.6 us (4%)
  local copies, waits for them, and re-layouts  5.12 us (1%)
    psum x1, waiting for transfers between devices, shards(): block_rows = lax.psum(jnp.dot(merged, basis, precision=HIGH), 'col')  86.3 us
    psum x1, waiting for transfers between devices, shards(): coeffs = lax.psum(coeff_part, 'row')  75 us
    another operation x6, other arithmetic, invert_gram(): factor = jnp.linalg.cholesky(gram_total)  34 us
    dot_general x1, matrix products, left_product(): lax.dot_general(block, factor_rows, (((0,), (0,)), ((), ())), precision=H...  32.2 us
    psum x1, waiting for transfers between devices, shards(): gram_total = lax.psum(gram_part, 'row')  31.4 us
    dot_general x1, matrix products, shards(): lax.dot_general(activations, out_grads, (((0,), (0,)), ((), ())), preferr...  29.5 us
    dot_general x1, matrix products, shards(): new_momentum = merged - 0.5 * jnp.dot(ortho, coeffs.T, precision=HIGH)  22.7 us
    psum x1, blocking collectives, shards(): sq_total = lax.psum(squares, 'col')  21.6 us
  transfers between devices with their start and end apart: 3, of which 3 were waited for; matrix products, arithmetic and copies ran while one was open for 0% of the time, Pallas kernels for 0%

commit v1 on v0

v1 whole, which is shorter than its diff:
```python
import math

import jax
import jax.numpy as jnp
from jax import lax
from jax.experimental import pallas as pl
from jax.experimental.pallas import tpu as pltpu
from jax.sharding import PartitionSpec as P


EPS = 1e-06
HIGH = lax.Precision.HIGHEST
F32 = jnp.float32
BF16 = jnp.bfloat16
LANES = 128
NN = (((1,), (0,)), ((), ()))
NT = (((1,), (1,)), ((), ()))


def split(x):
    hi = x.astype(BF16)
    return hi, (x - hi.astype(F32)).astype(BF16)


def dot(a, b, dims=NN):
    return lax.dot_general(a, b, dims, preferred_element_type=F32)


def params(flops, **kw):
    return dict(
        compiler_params=pltpu.CompilerParams(vmem_limit_bytes=56 * 2**20, **kw),
        cost_estimate=pl.CostEstimate(flops=flops, transcendentals=0, bytes_accessed=flops // 300),
    )


WIDE = 512


def joined3(left):
    return jnp.concatenate([left[0], left[1], left[0]], axis=1)


def front_kernel(momentum, activations, out_grads, basis, pieces):
    rows, cols = momentum.shape
    tokens, rank = out_grads.shape[0], basis.shape[1]
    high = rows // pieces
    wide = min(WIDE, cols)
    steps = pl.cdiv(cols, wide)
    last = cols - (steps - 1) * wide

    def body(mom_ref, act_ref, grad_ref, basis_ref, merged_ref, *rest):
        proj_refs, act_t = rest[:-1], rest[-1]
        step = pl.program_id(0)

        @pl.when(step == 0)
        def _():
            act_t[...] = act_ref[...].T
            for proj_ref in proj_refs:
                proj_ref[...] = jnp.zeros_like(proj_ref)

        def block(width):
            b_hi, b_lo = split(basis_ref[:width, :])
            right = jnp.concatenate([b_hi, b_hi, b_lo], axis=0)
            for k, proj_ref in enumerate(proj_refs):
                at = slice(k * high, (k + 1) * high)
                merged = mom_ref[at, :width] + dot(act_t[at, :], grad_ref[:, :width])
                merged_ref[at, :width] = merged
                proj_ref[...] += dot(joined3(split(merged)), right)

        if last == wide:
            block(wide)
        else:
            pl.when(step < steps - 1)(lambda: block(wide))
            pl.when(step == steps - 1)(lambda: block(last))

    return pl.pallas_call(
        body,
        grid=(steps,),
        in_specs=[
            pl.BlockSpec((rows, wide), lambda j: (0, j)),
            pl.BlockSpec((tokens, rows), lambda j: (0, 0)),
            pl.BlockSpec((tokens, wide), lambda j: (0, j)),
            pl.BlockSpec((wide, rank), lambda j: (j, 0)),
        ],
        out_specs=[pl.BlockSpec((rows, wide), lambda j: (0, j))]
        + [pl.BlockSpec((high, rank), lambda j: (0, 0))] * pieces,
        out_shape=[jax.ShapeDtypeStruct((rows, cols), F32)]
        + [jax.ShapeDtypeStruct((high, rank), F32)] * pieces,
        scratch_shapes=[pltpu.VMEM((rows, tokens), BF16)],
        name="front",
        **params(2 * rows * cols * (tokens + 3 * rank)),
    )(momentum, activations, out_grads, basis)


def gram_kernel(projected):
    rows, rank = projected.shape

    def body(proj_ref, gram_ref, turned_ref):
        value = proj_ref[...]
        hi, lo = split(value)
        t_hi, t_lo = hi.T, lo.T
        turned_ref[:rank, :] = t_hi
        turned_ref[rank:, :] = t_lo
        gram_ref[...] = dot(joined3((t_hi, t_lo)), jnp.concatenate([hi, hi, lo], axis=0))

    return pl.pallas_call(
        body,
        out_shape=[
            jax.ShapeDtypeStruct((rank, rank), F32),
            jax.ShapeDtypeStruct((2 * rank, rows), BF16),
        ],
        name="gram",
        **params(6 * rows * rank * rank),
    )(projected)


def right_kernel(merged, turned, start, span):
    rows = merged.shape[0]
    rank = turned.shape[0] // 2
    wide = min(WIDE, span)
    first = start // wide

    def body(merged_ref, turned_ref, out_ref):
        hi, lo = split(merged_ref[...])
        total = dot(turned_ref[...], hi)
        out_ref[...] = (total[:rank] + total[rank:] + dot(turned_ref[:rank, :], lo)).T

    return pl.pallas_call(
        body,
        grid=(pl.cdiv(span, wide),),
        in_specs=[
            pl.BlockSpec((rows, wide), lambda j: (0, first + j)),
            pl.BlockSpec((2 * rank, rows), lambda j: (0, 0)),
        ],
        out_specs=pl.BlockSpec((wide, rank), lambda j: (j, 0)),
        out_shape=jax.ShapeDtypeStruct((span, rank), F32),
        name="right",
        **params(6 * rows * span * rank),
    )(merged, turned)


def invert_base(block):
    size = block.shape[0]
    rows = [block[8 * g : 8 * g + 8, :] for g in range(size // 8)]
    lane = lax.broadcasted_iota(jnp.int32, (8, size), 1)
    sub = lax.broadcasted_iota(jnp.int32, (8, size), 0)
    for j in range(size):
        home, s = divmod(j, 8)
        column = jnp.broadcast_to(rows[home][:, j : j + 1], (8, size))
        pivot_row = rows[home][s : s + 1, :] / column[s : s + 1, :]
        pivot_inv = 1.0 / column[s : s + 1, :]
        here = lane == j
        pivot_row = jnp.broadcast_to(pivot_row, (8, size))
        pivot_inv = jnp.broadcast_to(pivot_inv, (8, size))
        for g in range(home, size // 8):
            if g > home:
                column = jnp.broadcast_to(rows[g][:, j : j + 1], (8, size))
            new = jnp.where(here, -column * pivot_inv, rows[g] - column * pivot_row)
            rows[g] = jnp.where(sub > s, new, rows[g]) if g == home else new
    out = []
    for g in range(size // 8):
        diagonal = lane == sub + 8 * g
        pivots = jnp.sum(jnp.where(diagonal, rows[g], 0.0), axis=1, keepdims=True)
        scale = 1.0 / jnp.sqrt(pivots)
        unit = jnp.where(lane < sub + 8 * g, rows[g], jnp.where(diagonal, 1.0, 0.0))
        out.append(unit * scale)
    return jnp.concatenate(out, axis=0)


def full_dot(a, b, dims=NN):
    return lax.dot_general(a, b, dims, precision=HIGH, preferred_element_type=F32)


def invert_factor(gram):
    size = gram.shape[0]
    if size <= LANES:
        return invert_base(gram)
    half = size // 2
    first = invert_factor(gram[:half, :half])
    below = full_dot(gram[half:, :half], first, NT)
    second = invert_factor(gram[half:, half:] - full_dot(below, below, NT))
    corner = -full_dot(second, full_dot(below, first))
    top = jnp.concatenate([first, jnp.zeros((half, size - half), F32)], axis=1)
    return jnp.concatenate([top, jnp.concatenate([corner, second], axis=1)], axis=0)


def ortho_kernel(gram, projected, root):
    rows, rank = projected.shape

    def body(gram_ref, proj_ref, inv_ref, left_ref, wide_ref):
        inverse = invert_factor(gram_ref[...])
        inv_ref[...] = inverse
        i_hi, i_lo = split(inverse)
        ortho = dot(joined3(split(proj_ref[...])), jnp.concatenate([i_hi, i_hi, i_lo], axis=1), NT)
        left_ref[...] = ortho * root
        wide_ref[...] = joined3(split(ortho))

    return pl.pallas_call(
        body,
        out_shape=[
            jax.ShapeDtypeStruct((rank, rank), F32),
            jax.ShapeDtypeStruct((rows, rank), F32),
            jax.ShapeDtypeStruct((rows, 3 * rank), BF16),
        ],
        name="ortho",
        **params(40 * 10**9),
    )(gram, projected)


def coeff_kernel(right, inverse):
    rows, rank = right.shape

    def body(right_ref, inv_ref, out_ref, sq_ref):
        i_hi, i_lo = split(inv_ref[...])
        coeffs = dot(joined3(split(right_ref[...])), jnp.concatenate([i_hi, i_hi, i_lo], axis=1), NT)
        out_ref[...] = coeffs
        sq_ref[...] = jnp.sum(coeffs * coeffs, axis=0, keepdims=True)

    return pl.pallas_call(
        body,
        out_shape=[jax.ShapeDtypeStruct((rows, rank), F32), jax.ShapeDtypeStruct((1, rank), F32)],
        name="coeff",
        **params(6 * rows * rank * rank),
    )(right, inverse)


def update_kernel(merged, wide_ortho, coeffs):
    rows, cols = merged.shape
    rank = coeffs[0].shape[1]
    wide = min(WIDE, cols)
    counts = [pl.cdiv(c.shape[0], wide) for c in coeffs]
    starts = [sum(counts[:k]) for k in range(len(counts))]
    chunks = len(coeffs)

    def body(ortho_ref, merged_ref, *rest):
        out_ref, turned_ref = rest[-2:]
        step = pl.program_id(0)
        for k in range(chunks):

            @pl.when((step >= starts[k]) & (step < starts[k] + counts[k]))
            def _(k=k):
                c_hi, c_lo = split(rest[k][...] * -0.5)
                turned_ref[...] = jnp.concatenate([c_hi, c_hi, c_lo], axis=1)

        out_ref[...] = merged_ref[...] + dot(ortho_ref[...], turned_ref[...], NT)

    def at(k):
        return lambda j: (jnp.clip(j - starts[k], 0, counts[k] - 1), 0)

    return pl.pallas_call(
        body,
        grid=(sum(counts),),
        in_specs=[
            pl.BlockSpec((rows, 3 * rank), lambda j: (0, 0)),
            pl.BlockSpec((rows, wide), lambda j: (0, j)),
        ]
        + [pl.BlockSpec((wide, rank), at(k)) for k in range(chunks)],
        out_specs=pl.BlockSpec((rows, wide), lambda j: (0, j)),
        out_shape=jax.ShapeDtypeStruct((rows, cols), F32),
        scratch_shapes=[pltpu.VMEM((wide, 3 * rank), BF16)],
        name="update",
        **params(6 * rows * cols * rank),
    )(wide_ortho, merged, *coeffs)


def swap(x, axis, size, bit):
    return lax.ppermute(x, axis, [(i, i ^ (1 << bit)) for i in range(size)])


def bits_of(size):
    bits = size.bit_length() - 1
    return bits if size == 1 << bits else None


def keep_and_send(x, mine):
    half = x.shape[0] // 2
    keep = lax.dynamic_slice_in_dim(x, mine * half, half, 0)
    send = lax.dynamic_slice_in_dim(x, (1 - mine) * half, half, 0)
    return keep, send


def join(own, other, mine):
    return jnp.where(mine == 0, jnp.concatenate([own, other], 0), jnp.concatenate([other, own], 0))


def reduce_all(x, axis, size, halved):
    bits = bits_of(size)
    if bits is None or x.shape[0] % (1 << len(halved)):
        return lax.psum(x, axis)
    at = lax.axis_index(axis)
    for bit in halved:
        keep, send = keep_and_send(x, (at >> bit) & 1)
        x = keep + swap(send, axis, size, bit)
    for bit in range(bits):
        if bit not in halved:
            x = x + swap(x, axis, size, bit)
    for bit in reversed(halved):
        x = join(x, swap(x, axis, size, bit), (at >> bit) & 1)
    return x


def solution(mesh):
    n_row, n_col = mesh.shape["row"], mesh.shape["col"]
    col_halved = list(range((bits_of(n_col) or 0) - 1))

    def spans_of(cols):
        return [2 * WIDE, 3 * WIDE, cols - 5 * WIDE] if cols > 6 * WIDE else [cols]

    def shards(momentum, activations, out_grads, basis):
        rows, cols = momentum.shape
        spans = spans_of(cols)
        merged, *parts = front_kernel(momentum, activations, out_grads, basis, 2)
        parts = [reduce_all(p, "col", n_col, col_halved) for p in parts]
        projected = jnp.concatenate(parts, axis=0)
        gram_part, turned = gram_kernel(projected)
        gram = reduce_all(gram_part, "row", n_row, [0])
        rights = []
        for k, span in enumerate(spans):
            part = right_kernel(merged, turned, sum(spans[:k]), span)
            rights.append(reduce_all(part, "row", n_row, [0]))
        inverse, left_basis, wide_ortho = ortho_kernel(gram, projected, math.sqrt(rows * n_row))
        pairs = [coeff_kernel(r, inverse) for r in rights]
        coeffs = [c for c, _ in pairs]
        squares = reduce_all(sum(s for _, s in pairs), "col", n_col, [])
        new_momentum = update_kernel(merged, wide_ortho, coeffs)
        inv_norm = lax.rsqrt(squares / (cols * n_col) + EPS)
        new_basis = jnp.concatenate([c * inv_norm for c in coeffs], axis=0)
        return new_momentum, left_basis, new_basis

    return jax.shard_map(
        shards,
        mesh=mesh,
        in_specs=(P("row", "col"), P(None, "row"), P(None, "col"), P("col", None)),
        out_specs=(P("row", "col"), P("row", None), P("col", None)),
        check_vma=False,
    )
```

time: 414 us -> 245 us (0.59); the launches traced: 406 us -> 244 us
  Pallas kernels: 0 us -> 117 us
  waiting for transfers between devices: 193 us -> 79.1 us
  matrix products: 111 us -> 0 us
  other arithmetic: 59.2 us -> 12 us
  starting transfers between devices: 0.29 us -> 27.9 us
  blocking collectives: 21.6 us -> 0 us
  between operations: 15.6 us -> 0.87 us
    psum x3 -> x0, waiting for transfers between devices: 193 us -> none  [the longest x1 86.3 us: shards(): block_rows = lax.psum(jnp.dot(merged, basis, precision=HIGH), 'col')]
    pallas_call x0 -> x10, Pallas kernels: none -> 117 us  [the longest x1 40.5 us: front_kernel(): pl.pallas_call(body, grid=(steps,), in_specs=[pl.BlockSpec((rows, wide),...]
    dot_general x6 -> x0, matrix products: 110 us -> none  [the longest x1 32.2 us: left_product(): lax.dot_general(block, factor_rows, (((0,), (0,)), ((), ())), precision=H...]
    ppermute x0 -> x25, waiting for transfers between devices: none -> 79.1 us  [swap(): return lax.ppermute(x, axis, [(i, i ^ 1 << bit) for i in range(size)])]
    another operation x9 -> x0, other arithmetic: 53.7 us -> none  [the longest x6 34 us: invert_gram(): factor = jnp.linalg.cholesky(gram_total)]
    ppermute x0 -> x25, starting transfers between devices: none -> 27.9 us  [swap(): return lax.ppermute(x, axis, [(i, i ^ 1 << bit) for i in range(size)])]
    psum x1 -> x0, blocking collectives: 21.6 us -> none  [shards(): sq_total = lax.psum(squares, 'col')]
    dynamic_slice x0 -> x8, local copies, waits for them, and re-layouts: none -> 4.6 us  [keep_and_send(): send = lax.dynamic_slice_in_dim(x, (1 - mine) * half, half, 0)]
  transfers between devices with their start and end apart: 3 -> 25, of which waited for: 3 -> 13; matrix products, arithmetic and copies ran while one was open for 0% -> 4% of each run, Pallas kernels for 0% -> 24%
where the time goes in v1:
time: 245 us; the launch traced here: 244 us
  Pallas kernels  117 us (48%)
  waiting for transfers between devices  79.1 us (32%)
  starting transfers between devices  27.9 us (11%)
  other arithmetic  12 us (5%)
  local copies, waits for them, and re-layouts  7.12 us (3%)
    ppermute x25, waiting for transfers between devices, swap(): return lax.ppermute(x, axis, [(i, i ^ 1 << bit) for i in range(size)])  79.1 us
    pallas_call x1, Pallas kernels, front_kernel(): pl.pallas_call(body, grid=(steps,), in_specs=[pl.BlockSpec((rows, wide),...  40.5 us
    ppermute x25, starting transfers between devices, swap(): return lax.ppermute(x, axis, [(i, i ^ 1 << bit) for i in range(size)])  27.9 us
    pallas_call x1, Pallas kernels, ortho_kernel(): pl.pallas_call(body, out_shape=[jax.ShapeDtypeStruct((rank, rank), F32),...  26.4 us
    pallas_call x1, Pallas kernels, update_kernel(): pl.pallas_call(body, grid=(sum(counts),), in_specs=[pl.BlockSpec((rows, 3...  19.9 us
    pallas_call x3, Pallas kernels, right_kernel(): pl.pallas_call(body, grid=(pl.cdiv(span, wide),), in_specs=[pl.BlockSpec(...  18.6 us
    pallas_call x3, Pallas kernels, coeff_kernel(): pl.pallas_call(body, out_shape=[jax.ShapeDtypeStruct((rows, rank), F32),...  9.01 us
  transfers between devices with their start and end apart: 25, of which 13 were waited for; matrix products, arithmetic and copies ran while one was open for 4% of the time, Pallas kernels for 24%

profile of v1, /device:TPU:0, one launch (start us, length us, event | category | flops | bytes accessed | tf_op | source)
XLA Modules:
  0.0 244.4 jit_solution(17045909010135707110)
XLA Ops:
  0.6 40.5 %front.1 = (f32[1280,3456]{1,0:T(8,128)}, f32[640,256]{1,0:T(8,128)}, f32[640,256]{1,0:T(8,128)}) custom-call(f32[1280,3456]{1,0:T(8,128)} %mom_ref.1, bf16[2048,1280]{1,0:T(8,128)(2,1)} %act_ref.1, bf16[2048,3456]{1,0:T(8,128)(2,1)} %grad_ref.1, f32[3456,256]{1,0:T(8,128)} %basis_ref.1), custom_call_target="tpu_custom_call" | custom-call | flops 24914165760 | bytes 83047216 | tf_op jit(solution)/shard_map/front/pallas_call | solution.py:76
  42.2 3.1 %collective-permute-start.5 = (f32[320,256]{1,0:T(8,128)S(1)}, f32[320,256]{1,0:T(8,128)S(1)}, u32[]{:S(2)}, u32[]{:S(2)}) collective-permute-start(f32[320,256]{1,0:T(8,128)S(1)} %constant_dynamic-slice_fusion.5), channel_id=1, source_target_pairs={{0,1},{1,0},{2,3},{3,2},{4,5},{5,4},{6,7},{7,6},{8,9},{9,8},{10,11... | collective-permute-start | bytes 983048 | tf_op jit(solution)/shard_map/ppermute | solution.py:267
  46.4 7.5 %collective-permute-done.5 = f32[320,256]{1,0:T(8,128)S(1)} collective-permute-done((f32[320,256]{1,0:T(8,128)S(1)}, f32[320,256]{1,0:T(8,128)S(1)}, u32[]{:S(2)}, u32[]{:S(2)}) %collective-permute-start.5) | collective-permute-done | bytes 327712 | tf_op jit(solution)/shard_map/ppermute | solution.py:267
  54.9 2.1 collective-permute-start.6
  57.0 3.0 %collective-permute-done = f32[320,256]{1,0:T(8,128)S(1)} collective-permute-done((f32[320,256]{1,0:T(8,128)S(1)}, f32[320,256]{1,0:T(8,128)S(1)}, u32[]{:S(2)}, u32[]{:S(2)}) %collective-permute-start) | collective-permute-done | bytes 327712 | tf_op jit(solution)/shard_map/ppermute | solution.py:267
  60.1 1.9 collective-permute-start.1
  62.0 2.7 %collective-permute-start.7 = (f32[160,256]{1,0:T(8,128)S(1)}, f32[160,256]{1,0:T(8,128)S(1)}, u32[]{:S(2)}, u32[]{:S(2)}) collective-permute-start(f32[160,256]{1,0:T(8,128)S(1)} %dynamic-slice_add_fusion.5), channel_id=1, source_target_pairs={{0,4},{1,5},{2,6},{3,7},{4,0},{5,1},{6,2},{7,3},{8,12},{9,13},{10,... | collective-permute-start | bytes 491528 | tf_op jit(solution)/shard_map/ppermute | solution.py:267
  64.6 3.3 %collective-permute-done.1 = f32[160,256]{1,0:T(8,128)S(1)} collective-permute-done((f32[160,256]{1,0:T(8,128)S(1)}, f32[160,256]{1,0:T(8,128)S(1)}, u32[]{:S(2)}, u32[]{:S(2)}) %collective-permute-start.1) | collective-permute-done | bytes 163872 | tf_op jit(solution)/shard_map/ppermute | solution.py:267
  68.0 1.9 collective-permute-start.2
  69.9 4.7 %collective-permute-done.7 = f32[160,256]{1,0:T(8,128)S(1)} collective-permute-done((f32[160,256]{1,0:T(8,128)S(1)}, f32[160,256]{1,0:T(8,128)S(1)}, u32[]{:S(2)}, u32[]{:S(2)}) %collective-permute-start.7) | collective-permute-done | bytes 163872 | tf_op jit(solution)/shard_map/ppermute | solution.py:267
  74.8 3.6 %collective-permute-done.2 = f32[160,256]{1,0:T(8,128)S(1)} collective-permute-done((f32[160,256]{1,0:T(8,128)S(1)}, f32[160,256]{1,0:T(8,128)S(1)}, u32[]{:S(2)}, u32[]{:S(2)}) %collective-permute-start.2) | collective-permute-done | bytes 163872 | tf_op jit(solution)/shard_map/ppermute | solution.py:267
  78.4 1.6 collective-permute-done.8
  80.1 1.6 collective-permute-start.9
  81.7 2.1 collective-permute-done.3
  83.8 1.6 collective-permute-start.4
  85.4 4.5 %collective-permute-done.9 = f32[320,256]{1,0:T(8,128)S(1)} collective-permute-done((f32[320,256]{1,0:T(8,128)S(1)}, f32[320,256]{1,0:T(8,128)S(1)}, u32[]{:S(2)}, u32[]{:S(2)}) %collective-permute-start.9) | collective-permute-done | bytes 327712 | tf_op jit(solution)/shard_map/ppermute | solution.py:267
  90.0 4.5 %collective-permute-done.4 = f32[320,256]{1,0:T(8,128)S(1)} collective-permute-done((f32[320,256]{1,0:T(8,128)S(1)}, f32[320,256]{1,0:T(8,128)S(1)}, u32[]{:S(2)}, u32[]{:S(2)}) %collective-permute-start.4) | collective-permute-done | bytes 327712 | tf_op jit(solution)/shard_map/ppermute | solution.py:267
  95.7 3.0 %gram.1 = (f32[256,256]{1,0:T(8,128)}, bf16[512,1280]{1,0:T(8,128)(2,1)}) custom-call(f32[1280,256]{1,0:T(8,128)} %pad_maximum_fusion.1.proj_ref), custom_call_target="tpu_custom_call" | custom-call | flops 503316480 | bytes 1677721 | tf_op jit(solution)/shard_map/gram/pallas_call | solution.py:106
  98.7 5.5 %right.5 = f32[896,256]{1,0:T(8,128)} custom-call(f32[1280,3456]{1,0:T(8,128)} %get-tuple-element.21.merged_ref, bf16[512,1280]{1,0:T(8,128)(2,1)} %get-tuple-element.22.turned_ref), custom_call_target="tpu_custom_call" | custom-call | flops 1761607680 | bytes 5872025 | tf_op jit(solution)/shard_map/right/pallas_call | solution.py:128
  104.2 7.5 %right.4 = f32[1536,256]{1,0:T(8,128)} custom-call(f32[1280,3456]{1,0:T(8,128)} %get-tuple-element.21.merged_ref, bf16[512,1280]{1,0:T(8,128)(2,1)} %get-tuple-element.22.turned_ref), custom_call_target="tpu_custom_call" | custom-call | flops 3019898880 | bytes 10066329 | tf_op jit(solution)/shard_map/right/pallas_call | solution.py:128
  113.7 5.6 %right.3 = f32[1024,256]{1,0:T(8,128)} custom-call(f32[1280,3456]{1,0:T(8,128)} %get-tuple-element.21.merged_ref, bf16[512,1280]{1,0:T(8,128)(2,1)} %get-tuple-element.22.turned_ref), custom_call_target="tpu_custom_call" | custom-call | flops 2013265920 | bytes 6710886 | tf_op jit(solution)/shard_map/right/pallas_call | solution.py:128
  126.8 39.0 %collective-permute-done.11 = f32[128,256]{1,0:T(8,128)S(1)} collective-permute-done((f32[128,256]{1,0:T(8,128)S(1)}, f32[128,256]{1,0:T(8,128)S(1)}, u32[]{:S(2)}, u32[]{:S(2)}) %collective-permute-start.11) | collective-permute-done | bytes 131104 | tf_op jit(solution)/shard_map/ppermute | solution.py:267
  170.1 26.4 %ortho.1 = (f32[256,256]{1,0:T(8,128)}, f32[1280,256]{1,0:T(8,128)}, bf16[1280,768]{1,0:T(8,128)(2,1)}) custom-call(f32[256,256]{1,0:T(8,128)} %maximum_select_fusion.7.gram_ref, f32[1280,256]{1,0:T(8,128)} %pad_maximum_fusion.1.proj_ref), custom_call_target="tpu_custom_call" | custom-call | flops 40000000000 | bytes 133333336 | tf_op jit(solution)/shard_map/ortho/pallas_call | solution.py:198
  197.4 2.7 %coeff.5 = (f32[896,256]{1,0:T(8,128)}, f32[1,256]{1,0:T(1,128)}) custom-call(f32[896,256]{1,0:T(8,128)} %maximum_select_fusion.2.right_ref, f32[256,256]{1,0:T(8,128)} %get-tuple-element.23.inv_ref), custom_call_target="tpu_custom_call" | custom-call | flops 352321536 | bytes 1174405 | tf_op jit(solution)/shard_map/coeff/pallas_call | solution.py:219
  201.2 2.9 %coeff.3 = (f32[1024,256]{1,0:T(8,128)}, f32[1,256]{1,0:T(1,128)}) custom-call(f32[1024,256]{1,0:T(8,128)} %maximum_select_fusion.1.right_ref, f32[256,256]{1,0:T(8,128)} %get-tuple-element.23.inv_ref), custom_call_target="tpu_custom_call" | custom-call | flops 402653184 | bytes 1342177 | tf_op jit(solution)/shard_map/coeff/pallas_call | solution.py:219
  205.4 3.4 %coeff.4 = (f32[1536,256]{1,0:T(8,128)}, f32[1,256]{1,0:T(1,128)}) custom-call(f32[1536,256]{1,0:T(8,128)} %maximum_select_fusion.right_ref, f32[256,256]{1,0:T(8,128)} %get-tuple-element.23.inv_ref), custom_call_target="tpu_custom_call" | custom-call | flops 603979776 | bytes 2013265 | tf_op jit(solution)/shard_map/coeff/pallas_call | solution.py:219
  211.0 2.1 collective-permute-done.22
  213.1 1.7 collective-permute-start.23
  214.8 1.9 collective-permute-done.23
  216.6 3.1 %collective-permute-start.24 = (f32[1,256]{1,0:T(1,128)S(1)}, f32[1,256]{1,0:T(1,128)S(1)}, u32[]{:S(2)}, u32[]{:S(2)}) collective-permute-start(f32[1,256]{1,0:T(1,128)S(1)} %add.132), channel_id=1, source_target_pairs={{0,4},{1,5},{2,6},{3,7},{4,0},{5,1},{6,2},{7,3},{8,12},{9,13},{10,... | collective-permute-start | bytes 3080 | tf_op jit(solution)/shard_map/ppermute | solution.py:267
  219.7 19.9 %update.1 = f32[1280,3456]{1,0:T(8,128)} custom-call(bf16[1280,768]{1,0:T(8,128)(2,1)} %get-tuple-element.20.ortho_ref, f32[1280,3456]{1,0:T(8,128)} %get-tuple-element.21.merged_ref, f32[1024,256]{1,0:T(8,128)} %get-tuple-element.24.rest_0_, f32[1536,256]{1,0:T(8,128)} %get-tuple-element.25.rest_1_, f32[896,256]{1,0:T(8,128)} %get-tuple-element.26.rest_2_), custom_call_target="tpu_custom_call" | custom-call | flops 6794772480 | bytes 22649240 | tf_op jit(solution)/shard_map/update/pallas_call | solution.py:250
  242.3 2.0 pad_maximum_fusion
  (87 shorter events, 26.7 us)
Async XLA Ops:
  41.1 18.9 %copy-start.6 = (f32[640,256]{1,0:T(8,128)S(1)}, f32[640,256]{1,0:T(8,128)}, u32[]{:S(2)}) copy-start(f32[640,256]{1,0:T(8,128)} %get-tuple-element.17) | copy-start | bytes 1966084
  42.2 11.6 %collective-permute-start.5 = (f32[320,256]{1,0:T(8,128)S(1)}, f32[320,256]{1,0:T(8,128)S(1)}, u32[]{:S(2)}, u32[]{:S(2)}) collective-permute-start(f32[320,256]{1,0:T(8,128)S(1)} %constant_dynamic-slice_fusion.5), channel_id=1, source_target_pairs={{0,1},{1,0},{2,3},{3,2},{4,5},{5,4},{6,7},{7,6},{8,9},{9,8},{10,11... | collective-permute-start | bytes 983048 | tf_op jit(solution)/shard_map/ppermute | solution.py:267
  46.3 13.7 %collective-permute-start = (f32[320,256]{1,0:T(8,128)S(1)}, f32[320,256]{1,0:T(8,128)S(1)}, u32[]{:S(2)}, u32[]{:S(2)}) collective-permute-start(f32[320,256]{1,0:T(8,128)S(1)} %constant_dynamic-slice_fusion.7), channel_id=1, source_target_pairs={{0,1},{1,0},{2,3},{3,2},{4,5},{5,4},{6,7},{7,6},{8,9},{9,8},{10,11... | collective-permute-start | bytes 983048 | tf_op jit(solution)/shard_map/ppermute | solution.py:267
  54.9 7.1 %collective-permute-start.6 = (f32[160,256]{1,0:T(8,128)S(1)}, f32[160,256]{1,0:T(8,128)S(1)}, u32[]{:S(2)}, u32[]{:S(2)}) collective-permute-start(f32[160,256]{1,0:T(8,128)S(1)} %constant_dynamic-slice_fusion.4), channel_id=1, source_target_pairs={{0,2},{1,3},{2,0},{3,1},{4,6},{5,7},{6,4},{7,5},{8,10},{9,11},{10,... | collective-permute-start | bytes 491528 | tf_op jit(solution)/shard_map/ppermute | solution.py:267
  60.1 7.9 %collective-permute-start.1 = (f32[160,256]{1,0:T(8,128)S(1)}, f32[160,256]{1,0:T(8,128)S(1)}, u32[]{:S(2)}, u32[]{:S(2)}) collective-permute-start(f32[160,256]{1,0:T(8,128)S(1)} %constant_dynamic-slice_fusion.6), channel_id=1, source_target_pairs={{0,2},{1,3},{2,0},{3,1},{4,6},{5,7},{6,4},{7,5},{8,10},{9,11},{10,... | collective-permute-start | bytes 491528 | tf_op jit(solution)/shard_map/ppermute | solution.py:267
  62.0 12.6 %collective-permute-start.7 = (f32[160,256]{1,0:T(8,128)S(1)}, f32[160,256]{1,0:T(8,128)S(1)}, u32[]{:S(2)}, u32[]{:S(2)}) collective-permute-start(f32[160,256]{1,0:T(8,128)S(1)} %dynamic-slice_add_fusion.5), channel_id=1, source_target_pairs={{0,4},{1,5},{2,6},{3,7},{4,0},{5,1},{6,2},{7,3},{8,12},{9,13},{10,... | collective-permute-start | bytes 491528 | tf_op jit(solution)/shard_map/ppermute | solution.py:267
  68.0 10.4 %collective-permute-start.2 = (f32[160,256]{1,0:T(8,128)S(1)}, f32[160,256]{1,0:T(8,128)S(1)}, u32[]{:S(2)}, u32[]{:S(2)}) collective-permute-start(f32[160,256]{1,0:T(8,128)S(1)} %dynamic-slice_add_fusion.6), channel_id=1, source_target_pairs={{0,4},{1,5},{2,6},{3,7},{4,0},{5,1},{6,2},{7,3},{8,12},{9,13},{10,... | collective-permute-start | bytes 491528 | tf_op jit(solution)/shard_map/ppermute | solution.py:267
  74.6 5.5 %collective-permute-start.8 = (f32[160,256]{1,0:T(8,128)S(1)}, f32[160,256]{1,0:T(8,128)S(1)}, u32[]{:S(2)}, u32[]{:S(2)}) collective-permute-start(f32[160,256]{1,0:T(8,128)S(1)} %add.112), channel_id=1, source_target_pairs={{0,2},{1,3},{2,0},{3,1},{4,6},{5,7},{6,4},{7,5},{8,10},{9,11},{10,... | collective-permute-start | bytes 491528 | tf_op jit(solution)/shard_map/ppermute | solution.py:267
  78.3 5.5 %collective-permute-start.3 = (f32[160,256]{1,0:T(8,128)S(1)}, f32[160,256]{1,0:T(8,128)S(1)}, u32[]{:S(2)}, u32[]{:S(2)}) collective-permute-start(f32[160,256]{1,0:T(8,128)S(1)} %add.109), channel_id=1, source_target_pairs={{0,2},{1,3},{2,0},{3,1},{4,6},{5,7},{6,4},{7,5},{8,10},{9,11},{10,... | collective-permute-start | bytes 491528 | tf_op jit(solution)/shard_map/ppermute | solution.py:267
  80.1 9.9 %collective-permute-start.9 = (f32[320,256]{1,0:T(8,128)S(1)}, f32[320,256]{1,0:T(8,128)S(1)}, u32[]{:S(2)}, u32[]{:S(2)}) collective-permute-start(f32[320,256]{1,0:T(8,128)S(1)} %maximum_select_fusion.6), channel_id=1, source_target_pairs={{0,1},{1,0},{2,3},{3,2},{4,5},{5,4},{6,7},{7,6},{8,9},{9,8},{10,11... | collective-permute-start | bytes 983048 | tf_op jit(solution)/shard_map/ppermute | solution.py:267
  83.8 10.6 %collective-permute-start.4 = (f32[320,256]{1,0:T(8,128)S(1)}, f32[320,256]{1,0:T(8,128)S(1)}, u32[]{:S(2)}, u32[]{:S(2)}) collective-permute-start(f32[320,256]{1,0:T(8,128)S(1)} %maximum_select_fusion.5), channel_id=1, source_target_pairs={{0,1},{1,0},{2,3},{3,2},{4,5},{5,4},{6,7},{7,6},{8,9},{9,8},{10,11... | collective-permute-start | bytes 983048 | tf_op jit(solution)/shard_map/ppermute | solution.py:267
  113.0 10.8 %collective-permute-start.16 = (f32[768,256]{1,0:T(8,128)S(1)}, f32[768,256]{1,0:T(8,128)S(1)}, u32[]{:S(2)}, u32[]{:S(2)}) collective-permute-start(f32[768,256]{1,0:T(8,128)S(1)} %constant_dynamic-slice_fusion.1), channel_id=1, source_target_pairs={{0,8},{8,0},{16,24},{24,16},{1,9},{9,1},{17,25},{25,17},{2,10},{10... | collective-permute-start | bytes 2359304 | tf_op jit(solution)/shard_map/ppermute | solution.py:267
  113.2 8.0 %collective-permute-start.19 = (f32[448,256]{1,0:T(8,128)S(1)}, f32[448,256]{1,0:T(8,128)}, u32[]{:S(2)}, u32[]{:S(2)}) collective-permute-start(f32[448,256]{1,0:T(8,128)S(1)} %constant_dynamic-slice_fusion), channel_id=1, source_target_pairs={{0,8},{8,0},{16,24},{24,16},{1,9},{9,1},{17,25},{25,17},{2,10},{10... | collective-permute-start | bytes 1376264 | tf_op jit(solution)/shard_map/ppermute | solution.py:267
  113.7 7.0 %copy-start.7 = (f32[256,256]{1,0:T(8,128)S(1)}, f32[256,256]{1,0:T(8,128)}, u32[]{:S(2)}) copy-start(f32[256,256]{1,0:T(8,128)} %get-tuple-element.19) | copy-start | bytes 786436
  119.3 4.5 %copy-start.1 = (f32[1536,256]{1,0:T(8,128)S(1)}, f32[1536,256]{1,0:T(8,128)}, u32[]{:S(2)}) copy-start(f32[1536,256]{1,0:T(8,128)} %right.4) | copy-start | bytes 4718596
  120.5 4.0 %collective-permute-start.13 = (f32[512,256]{1,0:T(8,128)S(1)}, f32[512,256]{1,0:T(8,128)S(1)}, u32[]{:S(2)}, u32[]{:S(2)}) collective-permute-start(f32[512,256]{1,0:T(8,128)S(1)} %constant_dynamic-slice_fusion.2), channel_id=1, source_target_pairs={{0,8},{8,0},{16,24},{24,16},{1,9},{9,1},{17,25},{25,17},{2,10},{10... | collective-permute-start | bytes 1572872 | tf_op jit(solution)/shard_map/ppermute | solution.py:267
  120.6 3.9 %copy-start.2 = (f32[1024,256]{1,0:T(8,128)S(1)}, f32[1024,256]{1,0:T(8,128)}, u32[]{:S(2)}) copy-start(f32[1024,256]{1,0:T(8,128)} %right.3) | copy-start | bytes 3145732
  120.6 5.5 %collective-permute-start.10 = (f32[128,256]{1,0:T(8,128)S(1)}, f32[128,256]{1,0:T(8,128)S(1)}, u32[]{:S(2)}, u32[]{:S(2)}) collective-permute-start(f32[128,256]{1,0:T(8,128)S(1)} %constant_dynamic-slice_fusion.3), channel_id=1, source_target_pairs={{0,8},{8,0},{16,24},{24,16},{1,9},{9,1},{17,25},{25,17},{2,10},{10... | collective-permute-start | bytes 393224 | tf_op jit(solution)/shard_map/ppermute | solution.py:267
  122.2 45.7 %collective-permute-start.20 = (f32[448,256]{1,0:T(8,128)S(1)}, f32[448,256]{1,0:T(8,128)}, u32[]{:S(2)}, u32[]{:S(2)}) collective-permute-start(f32[448,256]{1,0:T(8,128)S(1)} %dynamic-slice_add_fusion.2), channel_id=1, source_target_pairs={{0,16},{8,24},{16,0},{24,8},{1,17},{9,25},{17,1},{25,9},{2,18},{10... | collective-permute-start | bytes 1376264 | tf_op jit(solution)/shard_map/ppermute | solution.py:267
  123.9 45.9 %collective-permute-start.17 = (f32[768,256]{1,0:T(8,128)S(1)}, f32[768,256]{1,0:T(8,128)S(1)}, u32[]{:S(2)}, u32[]{:S(2)}) collective-permute-start(f32[768,256]{1,0:T(8,128)S(1)} %dynamic-slice_add_fusion), channel_id=1, source_target_pairs={{0,16},{8,24},{16,0},{24,8},{1,17},{9,25},{17,1},{25,9},{2,18},{10... | collective-permute-start | bytes 2359304 | tf_op jit(solution)/shard_map/ppermute | solution.py:267
  124.6 44.7 %collective-permute-start.14 = (f32[512,256]{1,0:T(8,128)S(1)}, f32[512,256]{1,0:T(8,128)S(1)}, u32[]{:S(2)}, u32[]{:S(2)}) collective-permute-start(f32[512,256]{1,0:T(8,128)S(1)} %dynamic-slice_add_fusion.1), channel_id=1, source_target_pairs={{0,16},{8,24},{16,0},{24,8},{1,17},{9,25},{17,1},{25,9},{2,18},{10... | collective-permute-start | bytes 1572872 | tf_op jit(solution)/shard_map/ppermute | solution.py:267
  126.1 39.6 %collective-permute-start.11 = (f32[128,256]{1,0:T(8,128)S(1)}, f32[128,256]{1,0:T(8,128)S(1)}, u32[]{:S(2)}, u32[]{:S(2)}) collective-permute-start(f32[128,256]{1,0:T(8,128)S(1)} %dynamic-slice_add_fusion.7), channel_id=1, source_target_pairs={{0,16},{8,24},{16,0},{24,8},{1,17},{9,25},{17,1},{25,9},{2,18},{10... | collective-permute-start | bytes 393224 | tf_op jit(solution)/shard_map/ppermute | solution.py:267
  165.8 1.4 collective-permute-start.12
  169.0 27.4 %collective-permute-start.21 = (f32[448,256]{1,0:T(8,128)S(1)}, f32[448,256]{1,0:T(8,128)S(1)}, u32[]{:S(2)}, u32[]{:S(2)}) collective-permute-start(f32[448,256]{1,0:T(8,128)S(1)} %add.128), channel_id=1, source_target_pairs={{0,8},{8,0},{16,24},{24,16},{1,9},{9,1},{17,25},{25,17},{2,10},{10... | collective-permute-start | bytes 1376264 | tf_op jit(solution)/shard_map/ppermute | solution.py:267
  169.3 30.9 %collective-permute-start.15 = (f32[512,256]{1,0:T(8,128)S(1)}, f32[512,256]{1,0:T(8,128)S(1)}, u32[]{:S(2)}, u32[]{:S(2)}) collective-permute-start(f32[512,256]{1,0:T(8,128)S(1)} %add.120), channel_id=1, source_target_pairs={{0,8},{8,0},{16,24},{24,16},{1,9},{9,1},{17,25},{25,17},{2,10},{10... | collective-permute-start | bytes 1572872 | tf_op jit(solution)/shard_map/ppermute | solution.py:267
  169.8 34.3 %collective-permute-start.18 = (f32[768,256]{1,0:T(8,128)S(1)}, f32[768,256]{1,0:T(8,128)S(1)}, u32[]{:S(2)}, u32[]{:S(2)}) collective-permute-start(f32[768,256]{1,0:T(8,128)S(1)} %add.124), channel_id=1, source_target_pairs={{0,8},{8,0},{16,24},{24,16},{1,9},{9,1},{17,25},{25,17},{2,10},{10... | collective-permute-start | bytes 2359304 | tf_op jit(solution)/shard_map/ppermute | solution.py:267
  205.4 3.4 %copy-start.8 = (f32[1,256]{1,0:T(1,128)S(1)}, f32[1,256]{1,0:T(1,128)}, u32[]{:S(2)}) copy-start(f32[1,256]{1,0:T(1,128)} %get-tuple-element.30) | copy-start | bytes 3076
  205.4 3.4 %copy-start.9 = (f32[1,256]{1,0:T(1,128)S(1)}, f32[1,256]{1,0:T(1,128)}, u32[]{:S(2)}) copy-start(f32[1,256]{1,0:T(1,128)} %get-tuple-element.28) | copy-start | bytes 3076
  209.5 3.6 %collective-permute-start.22 = (f32[1,256]{1,0:T(1,128)S(1)}, f32[1,256]{1,0:T(1,128)S(1)}, u32[]{:S(2)}, u32[]{:S(2)}) collective-permute-start(f32[1,256]{1,0:T(1,128)S(1)} %add_add_fusion), channel_id=1, source_target_pairs={{0,1},{1,0},{2,3},{3,2},{4,5},{5,4},{6,7},{7,6},{8,9},{9,8},{10,11... | collective-permute-start | bytes 3080 | tf_op jit(solution)/shard_map/ppermute | solution.py:267
  213.1 3.6 %collective-permute-start.23 = (f32[1,256]{1,0:T(1,128)S(1)}, f32[1,256]{1,0:T(1,128)S(1)}, u32[]{:S(2)}, u32[]{:S(2)}) collective-permute-start(f32[1,256]{1,0:T(1,128)S(1)} %add.131), channel_id=1, source_target_pairs={{0,2},{1,3},{2,0},{3,1},{4,6},{5,7},{6,4},{7,5},{8,10},{9,11},{10,... | collective-permute-start | bytes 3080 | tf_op jit(solution)/shard_map/ppermute | solution.py:267
  216.6 23.0 %collective-permute-start.24 = (f32[1,256]{1,0:T(1,128)S(1)}, f32[1,256]{1,0:T(1,128)S(1)}, u32[]{:S(2)}, u32[]{:S(2)}) collective-permute-start(f32[1,256]{1,0:T(1,128)S(1)} %add.132), channel_id=1, source_target_pairs={{0,4},{1,5},{2,6},{3,7},{4,0},{5,1},{6,2},{7,3},{8,12},{9,13},{10,... | collective-permute-start | bytes 3080 | tf_op jit(solution)/shard_map/ppermute | solution.py:267
  219.7 19.9 %copy-start.4 = (f32[896,256]{1,0:T(8,128)S(1)}, f32[896,256]{1,0:T(8,128)}, u32[]{:S(2)}) copy-start(f32[896,256]{1,0:T(8,128)} %get-tuple-element.26.rest_2_) | copy-start | bytes 2752516
  (3 other events, 4.0 us)

commit v2 on v1

--- a/solution.py
+++ b/solution.py
@@ -26,9 +26,9 @@
     return lax.dot_general(a, b, dims, preferred_element_type=F32)
 
 
-def params(flops, **kw):
+def params(flops, room=20, **kw):
     return dict(
-        compiler_params=pltpu.CompilerParams(vmem_limit_bytes=56 * 2**20, **kw),
+        compiler_params=pltpu.CompilerParams(vmem_limit_bytes=room * 2**20, **kw),
         cost_estimate=pl.CostEstimate(flops=flops, transcendentals=0, bytes_accessed=flops // 300),
     )
 
@@ -64,7 +64,7 @@
             for k, proj_ref in enumerate(proj_refs):
                 at = slice(k * high, (k + 1) * high)
                 merged = mom_ref[at, :width] + dot(act_t[at, :], grad_ref[:, :width])
-                merged_ref[at, :width] = merged
+                merged_ref[at, pl.ds(pl.multiple_of(step * wide, wide), width)] = merged
                 proj_ref[...] += dot(joined3(split(merged)), right)
 
         if last == wide:
@@ -82,13 +82,13 @@
             pl.BlockSpec((tokens, wide), lambda j: (0, j)),
             pl.BlockSpec((wide, rank), lambda j: (j, 0)),
         ],
-        out_specs=[pl.BlockSpec((rows, wide), lambda j: (0, j))]
+        out_specs=[pl.BlockSpec(memory_space=pltpu.VMEM)]
         + [pl.BlockSpec((high, rank), lambda j: (0, 0))] * pieces,
-        out_shape=[jax.ShapeDtypeStruct((rows, cols), F32)]
+        out_shape=[pltpu.VMEM((rows, cols), F32)]
         + [jax.ShapeDtypeStruct((high, rank), F32)] * pieces,
         scratch_shapes=[pltpu.VMEM((rows, tokens), BF16)],
         name="front",
-        **params(2 * rows * cols * (tokens + 3 * rank)),
+        **params(2 * rows * cols * (tokens + 3 * rank), 40),
     )(momentum, activations, out_grads, basis)
 
 
@@ -118,21 +118,17 @@
     rows = merged.shape[0]
     rank = turned.shape[0] // 2
     wide = min(WIDE, span)
-    first = start // wide
 
     def body(merged_ref, turned_ref, out_ref):
-        hi, lo = split(merged_ref[...])
-        total = dot(turned_ref[...], hi)
-        out_ref[...] = (total[:rank] + total[rank:] + dot(turned_ref[:rank, :], lo)).T
-
-    return pl.pallas_call(
-        body,
-        grid=(pl.cdiv(span, wide),),
-        in_specs=[
-            pl.BlockSpec((rows, wide), lambda j: (0, first + j)),
-            pl.BlockSpec((2 * rank, rows), lambda j: (0, 0)),
-        ],
-        out_specs=pl.BlockSpec((wide, rank), lambda j: (j, 0)),
+        for at in range(0, span, wide):
+            width = min(wide, span - at)
+            hi, lo = split(merged_ref[:, start + at : start + at + width])
+            total = dot(turned_ref[...], hi)
+            out_ref[at : at + width, :] = (total[:rank] + total[rank:] + dot(turned_ref[:rank, :], lo)).T
+
+    return pl.pallas_call(
+        body,
+        in_specs=[pl.BlockSpec(memory_space=pltpu.VMEM)] * 2,
         out_shape=jax.ShapeDtypeStruct((span, rank), F32),
         name="right",
         **params(6 * rows * span * rank),
@@ -144,26 +140,37 @@
     rows = [block[8 * g : 8 * g + 8, :] for g in range(size // 8)]
     lane = lax.broadcasted_iota(jnp.int32, (8, size), 1)
     sub = lax.broadcasted_iota(jnp.int32, (8, size), 0)
-    for j in range(size):
-        home, s = divmod(j, 8)
-        column = jnp.broadcast_to(rows[home][:, j : j + 1], (8, size))
-        pivot_row = rows[home][s : s + 1, :] / column[s : s + 1, :]
-        pivot_inv = 1.0 / column[s : s + 1, :]
-        here = lane == j
-        pivot_row = jnp.broadcast_to(pivot_row, (8, size))
-        pivot_inv = jnp.broadcast_to(pivot_inv, (8, size))
+
+    def spread(value):
+        return jnp.broadcast_to(value, (8, size))
+
+    for start in range(0, size, 4):
+        home, offset = divmod(start, 8)
+        inverses, pivots, factors = [], [], {}
         for g in range(home, size // 8):
-            if g > home:
-                column = jnp.broadcast_to(rows[g][:, j : j + 1], (8, size))
-            new = jnp.where(here, -column * pivot_inv, rows[g] - column * pivot_row)
-            rows[g] = jnp.where(sub > s, new, rows[g]) if g == home else new
+            columns = [spread(rows[g][:, start + t : start + t + 1]) for t in range(4)]
+            row = rows[g]
+            for t in range(4):
+                s = offset + t
+                if g == home:
+                    inverse = 1.0 / columns[t][s : s + 1, :]
+                    inverses.append(spread(inverse))
+                    pivots.append(spread(row[s : s + 1, :] * inverse))
+                    for u in range(t + 1, 4):
+                        factors[t, u] = spread(columns[u][s : s + 1, :] * inverse)
+                below = sub > s
+                for u in range(t + 1, 4):
+                    new = columns[u] - columns[t] * factors[t, u]
+                    columns[u] = jnp.where(below, new, columns[u]) if g == home else new
+                new = jnp.where(lane == start + t, -columns[t] * inverses[t], row - columns[t] * pivots[t])
+                row = jnp.where(below, new, row) if g == home else new
+            rows[g] = row
     out = []
     for g in range(size // 8):
         diagonal = lane == sub + 8 * g
-        pivots = jnp.sum(jnp.where(diagonal, rows[g], 0.0), axis=1, keepdims=True)
-        scale = 1.0 / jnp.sqrt(pivots)
+        found = jnp.sum(jnp.where(diagonal, rows[g], 0.0), axis=1, keepdims=True)
         unit = jnp.where(lane < sub + 8 * g, rows[g], jnp.where(diagonal, 1.0, 0.0))
-        out.append(unit * scale)
+        out.append(unit * (1.0 / jnp.sqrt(found)))
     return jnp.concatenate(out, axis=0)
 
 
@@ -224,43 +231,45 @@
     )(right, inverse)
 
 
-def update_kernel(merged, wide_ortho, coeffs):
+def update_kernel(merged, wide_ortho, coeffs, start, earlier):
     rows, cols = merged.shape
-    rank = coeffs[0].shape[1]
-    wide = min(WIDE, cols)
-    counts = [pl.cdiv(c.shape[0], wide) for c in coeffs]
-    starts = [sum(counts[:k]) for k in range(len(counts))]
-    chunks = len(coeffs)
-
-    def body(ortho_ref, merged_ref, *rest):
-        out_ref, turned_ref = rest[-2:]
+    span, rank = coeffs.shape
+    wide = min(WIDE, span)
+    first, steps = start // wide, pl.cdiv(span, wide)
+    last = span - (steps - 1) * wide
+
+    def body(ortho_ref, merged_ref, coeff_ref, *rest):
+        out_ref = rest[-1]
         step = pl.program_id(0)
-        for k in range(chunks):
-
-            @pl.when((step >= starts[k]) & (step < starts[k] + counts[k]))
-            def _(k=k):
-                c_hi, c_lo = split(rest[k][...] * -0.5)
-                turned_ref[...] = jnp.concatenate([c_hi, c_hi, c_lo], axis=1)
-
-        out_ref[...] = merged_ref[...] + dot(ortho_ref[...], turned_ref[...], NT)
-
-    def at(k):
-        return lambda j: (jnp.clip(j - starts[k], 0, counts[k] - 1), 0)
-
-    return pl.pallas_call(
-        body,
-        grid=(sum(counts),),
+
+        def block(width):
+            c_hi, c_lo = split(coeff_ref[:width, :] * -0.5)
+            fix = dot(ortho_ref[...], jnp.concatenate([c_hi, c_hi, c_lo], axis=1), NT)
+            at = pl.multiple_of((first + step) * wide, wide)
+            out_ref[:, :width] = merged_ref[:, pl.ds(at, width)] + fix
+
+        if last == wide:
+            block(wide)
+        else:
+            pl.when(step < steps - 1)(lambda: block(wide))
+            pl.when(step == steps - 1)(lambda: block(last))
+
+    more = [] if earlier is None else [earlier]
+    return pl.pallas_call(
+        body,
+        grid=(steps,),
         in_specs=[
             pl.BlockSpec((rows, 3 * rank), lambda j: (0, 0)),
-            pl.BlockSpec((rows, wide), lambda j: (0, j)),
+            pl.BlockSpec(memory_space=pltpu.VMEM),
+            pl.BlockSpec((wide, rank), lambda j: (j, 0)),
         ]
-        + [pl.BlockSpec((wide, rank), at(k)) for k in range(chunks)],
-        out_specs=pl.BlockSpec((rows, wide), lambda j: (0, j)),
+        + [pl.BlockSpec(memory_space=pl.ANY) for _ in more],
+        out_specs=pl.BlockSpec((rows, wide), lambda j: (0, first + j)),
         out_shape=jax.ShapeDtypeStruct((rows, cols), F32),
-        scratch_shapes=[pltpu.VMEM((wide, 3 * rank), BF16)],
+        input_output_aliases={3: 0} if more else {},
         name="update",
-        **params(6 * rows * cols * rank),
-    )(wide_ortho, merged, *coeffs)
+        **params(6 * rows * span * rank),
+    )(wide_ortho, merged, coeffs, *more)
 
 
 def swap(x, axis, size, bit):
@@ -274,28 +283,36 @@
 
 def keep_and_send(x, mine):
     half = x.shape[0] // 2
-    keep = lax.dynamic_slice_in_dim(x, mine * half, half, 0)
-    send = lax.dynamic_slice_in_dim(x, (1 - mine) * half, half, 0)
+    keep = lax.dynamic_slice(x, (mine[half], mine[0]), (half, x.shape[1]), allow_negative_indices=False)
+    send = lax.dynamic_slice(x, (mine[-half], mine[0]), (half, x.shape[1]), allow_negative_indices=False)
     return keep, send
 
 
 def join(own, other, mine):
-    return jnp.where(mine == 0, jnp.concatenate([own, other], 0), jnp.concatenate([other, own], 0))
-
-
-def reduce_all(x, axis, size, halved):
+    return jnp.where(mine["low"], jnp.concatenate([own, other], 0), jnp.concatenate([other, own], 0))
+
+
+def bit_table(axis, bit, halves):
+    mine = (lax.axis_index(axis) >> bit) & 1
+    table = {0: jnp.zeros((), jnp.int32), "low": mine == 0}
+    for half in halves:
+        table[half] = mine * half
+        table[-half] = (1 - mine) * half
+    return table
+
+
+def reduce_all(x, axis, size, halved, tables):
     bits = bits_of(size)
     if bits is None or x.shape[0] % (1 << len(halved)):
         return lax.psum(x, axis)
-    at = lax.axis_index(axis)
     for bit in halved:
-        keep, send = keep_and_send(x, (at >> bit) & 1)
+        keep, send = keep_and_send(x, tables[axis, bit])
         x = keep + swap(send, axis, size, bit)
     for bit in range(bits):
         if bit not in halved:
             x = x + swap(x, axis, size, bit)
     for bit in reversed(halved):
-        x = join(x, swap(x, axis, size, bit), (at >> bit) & 1)
+        x = join(x, swap(x, axis, size, bit), tables[axis, bit])
     return x
 
 
@@ -309,20 +326,29 @@
     def shards(momentum, activations, out_grads, basis):
         rows, cols = momentum.shape
         spans = spans_of(cols)
+        rank = basis.shape[1]
+        tables = {("col", b): bit_table("col", b, [rows // 4 >> i for i in range(len(col_halved))]) for b in col_halved}
+        tables["row", 0] = bit_table("row", 0, sorted({s // 2 for s in [rank, *spans]}))
+        keys = [(t, k) for t in tables for k in tables[t]]
+        momentum, *flat = lax.optimization_barrier((momentum, *[tables[t][k] for t, k in keys]))
+        for (t, k), value in zip(keys, flat):
+            tables[t][k] = value
         merged, *parts = front_kernel(momentum, activations, out_grads, basis, 2)
-        parts = [reduce_all(p, "col", n_col, col_halved) for p in parts]
+        parts = [reduce_all(p, "col", n_col, col_halved, tables) for p in parts]
         projected = jnp.concatenate(parts, axis=0)
         gram_part, turned = gram_kernel(projected)
-        gram = reduce_all(gram_part, "row", n_row, [0])
+        gram = reduce_all(gram_part, "row", n_row, [0], tables)
         rights = []
         for k, span in enumerate(spans):
             part = right_kernel(merged, turned, sum(spans[:k]), span)
-            rights.append(reduce_all(part, "row", n_row, [0]))
+            rights.append(reduce_all(part, "row", n_row, [0], tables))
         inverse, left_basis, wide_ortho = ortho_kernel(gram, projected, math.sqrt(rows * n_row))
         pairs = [coeff_kernel(r, inverse) for r in rights]
         coeffs = [c for c, _ in pairs]
-        squares = reduce_all(sum(s for _, s in pairs), "col", n_col, [])
-        new_momentum = update_kernel(merged, wide_ortho, coeffs)
+        squares = reduce_all(sum(s for _, s in pairs), "col", n_col, [], tables)
+        new_momentum = None
+        for k, c in enumerate(coeffs):
+            new_momentum = update_kernel(merged, wide_ortho, c, sum(spans[:k]), new_momentum)
         inv_norm = lax.rsqrt(squares / (cols * n_col) + EPS)
         new_basis = jnp.concatenate([c * inv_norm for c in coeffs], axis=0)
         return new_momentum, left_basis, new_basis

time: 245 us -> 187 us (0.76)
  Pallas kernels: 117 us -> 75.8 us
  other arithmetic: 12 us -> 4.48 us
  local copies, waits for them, and re-layouts: 7.12 us -> 2.31 us
  waiting for transfers between devices: 79.1 us -> 75.1 us
    pallas_call x4 -> x6, Pallas kernels: 38.5 us -> 21.1 us  [the longest x3 13.2 us: update_kernel(): pl.pallas_call(body, grid=(steps,), in_specs=[pl.BlockSpec((rows, 3 * ran...]
    pallas_call x1, Pallas kernels: 26.4 us -> 12.1 us  [ortho_kernel(): pl.pallas_call(body, out_shape=[jax.ShapeDtypeStruct((rank, rank), F32),...]
    pallas_call x3, Pallas kernels: 9.01 us -> 2.07 us  [coeff_kernel(): pl.pallas_call(body, out_shape=[jax.ShapeDtypeStruct((rows, rank), F32),...]
    ppermute x25, waiting for transfers between devices: 79.1 us -> 75.1 us  [swap(): return lax.ppermute(x, axis, [(i, i ^ 1 << bit) for i in range(size)])]
    select_n x8, other arithmetic: 4.21 us -> 0.44 us  [join(): jnp.where(mine['low'], jnp.concatenate([own, other], 0), jnp.concatenate(...]
    unnamed x20 -> x2, local copies, waits for them, and re-layouts: 2.52 us -> 0.01 us
  transfers between devices with their start and end apart: 25 -> 25, of which waited for: 13 -> 11; matrix products, arithmetic and copies ran while one was open for 4% -> 2% of each run, Pallas kernels for 24% -> 15%
where the time goes in v2:
time: 187 us
  Pallas kernels  75.8 us (41%)
  waiting for transfers between devices  75.1 us (40%)
  starting transfers between devices  28.5 us (15%)
  other arithmetic  4.48 us (2%)
  local copies, waits for them, and re-layouts  2.31 us (1%)
    ppermute x25, waiting for transfers between devices, swap(): return lax.ppermute(x, axis, [(i, i ^ 1 << bit) for i in range(size)])  75.1 us
    pallas_call x1, Pallas kernels, front_kernel(): pl.pallas_call(body, grid=(steps,), in_specs=[pl.BlockSpec((rows, wide),...  39.7 us
    ppermute x25, starting transfers between devices, swap(): return lax.ppermute(x, axis, [(i, i ^ 1 << bit) for i in range(size)])  28.5 us
    pallas_call x3, Pallas kernels, update_kernel(): pl.pallas_call(body, grid=(steps,), in_specs=[pl.BlockSpec((rows, 3 * ran...  13.2 us
    pallas_call x1, Pallas kernels, ortho_kernel(): pl.pallas_call(body, out_shape=[jax.ShapeDtypeStruct((rank, rank), F32),...  12.1 us
    pallas_call x3, Pallas kernels, right_kernel(): pl.pallas_call(body, in_specs=[pl.BlockSpec(memory_space=pltpu.VMEM)] * 2...  7.96 us
  transfers between devices with their start and end apart: 25, of which 11 were waited for; matrix products, arithmetic and copies ran while one was open for 2% of the time, Pallas kernels for 15%

profile of v2, /device:TPU:0, one launch (start us, length us, event | category | flops | bytes accessed | tf_op | source)
XLA Modules:
  0.0 187.2 jit_solution(18337133958270168474)
XLA Ops:
  0.7 39.7 %front.1 = (f32[1280,3456]{1,0:T(8,128)S(1)}, f32[640,256]{1,0:T(8,128)}, f32[640,256]{1,0:T(8,128)}) custom-call(f32[1280,3456]{1,0:T(8,128)} %mom_ref, bf16[2048,1280]{1,0:T(8,128)(2,1)} %act_ref.1, bf16[2048,3456]{1,0:T(8,128)(2,1)} %grad_ref.1, f32[3456,256]{1,0:T(8,128)} %basis_ref.1), custom_call_target="tpu_custom_call" | custom-call | flops 24914165760 | bytes 83047216 | tf_op jit(solution)/shard_map/front/pallas_call | solution.py:76
  41.4 3.1 %collective-permute-start.5 = (f32[320,256]{1,0:T(8,128)S(1)}, f32[320,256]{1,0:T(8,128)S(1)}, u32[]{:S(2)}, u32[]{:S(2)}) collective-permute-start(f32[320,256]{1,0:T(8,128)S(1)} %constant_dynamic-slice_fusion.5), channel_id=1, source_target_pairs={{0,1},{1,0},{2,3},{3,2},{4,5},{5,4},{6,7},{7,6},{8,9},{9,8},{10,11... | collective-permute-start | bytes 983048 | tf_op jit(solution)/shard_map/ppermute | solution.py:276
  45.6 7.5 %collective-permute-done.5 = f32[320,256]{1,0:T(8,128)S(1)} collective-permute-done((f32[320,256]{1,0:T(8,128)S(1)}, f32[320,256]{1,0:T(8,128)S(1)}, u32[]{:S(2)}, u32[]{:S(2)}) %collective-permute-start.5) | collective-permute-done | bytes 327712 | tf_op jit(solution)/shard_map/ppermute | solution.py:276
  54.1 2.1 %collective-permute-start.6 = (f32[160,256]{1,0:T(8,128)S(1)}, f32[160,256]{1,0:T(8,128)S(1)}, u32[]{:S(2)}, u32[]{:S(2)}) collective-permute-start(f32[160,256]{1,0:T(8,128)S(1)} %constant_dynamic-slice_fusion.4), channel_id=1, source_target_pairs={{0,2},{1,3},{2,0},{3,1},{4,6},{5,7},{6,4},{7,5},{8,10},{9,11},{10,... | collective-permute-start | bytes 491528 | tf_op jit(solution)/shard_map/ppermute | solution.py:276
  56.3 3.0 %collective-permute-done = f32[320,256]{1,0:T(8,128)S(1)} collective-permute-done((f32[320,256]{1,0:T(8,128)S(1)}, f32[320,256]{1,0:T(8,128)S(1)}, u32[]{:S(2)}, u32[]{:S(2)}) %collective-permute-start) | collective-permute-done | bytes 327712 | tf_op jit(solution)/shard_map/ppermute | solution.py:276
  59.3 1.9 collective-permute-start.1
  61.2 2.7 %collective-permute-start.7 = (f32[160,256]{1,0:T(8,128)S(1)}, f32[160,256]{1,0:T(8,128)S(1)}, u32[]{:S(2)}, u32[]{:S(2)}) collective-permute-start(f32[160,256]{1,0:T(8,128)S(1)} %dynamic-slice_add_fusion.5), channel_id=1, source_target_pairs={{0,4},{1,5},{2,6},{3,7},{4,0},{5,1},{6,2},{7,3},{8,12},{9,13},{10,... | collective-permute-start | bytes 491528 | tf_op jit(solution)/shard_map/ppermute | solution.py:276
  63.9 3.3 %collective-permute-done.1 = f32[160,256]{1,0:T(8,128)S(1)} collective-permute-done((f32[160,256]{1,0:T(8,128)S(1)}, f32[160,256]{1,0:T(8,128)S(1)}, u32[]{:S(2)}, u32[]{:S(2)}) %collective-permute-start.1) | collective-permute-done | bytes 163872 | tf_op jit(solution)/shard_map/ppermute | solution.py:276
  67.2 1.9 %collective-permute-start.2 = (f32[160,256]{1,0:T(8,128)S(1)}, f32[160,256]{1,0:T(8,128)S(1)}, u32[]{:S(2)}, u32[]{:S(2)}) collective-permute-start(f32[160,256]{1,0:T(8,128)S(1)} %dynamic-slice_add_fusion.6), channel_id=1, source_target_pairs={{0,4},{1,5},{2,6},{3,7},{4,0},{5,1},{6,2},{7,3},{8,12},{9,13},{10,... | collective-permute-start | bytes 491528 | tf_op jit(solution)/shard_map/ppermute | solution.py:276
  69.1 4.8 %collective-permute-done.7 = f32[160,256]{1,0:T(8,128)S(1)} collective-permute-done((f32[160,256]{1,0:T(8,128)S(1)}, f32[160,256]{1,0:T(8,128)S(1)}, u32[]{:S(2)}, u32[]{:S(2)}) %collective-permute-start.7) | collective-permute-done | bytes 163872 | tf_op jit(solution)/shard_map/ppermute | solution.py:276
  74.0 3.5 %collective-permute-done.2 = f32[160,256]{1,0:T(8,128)S(1)} collective-permute-done((f32[160,256]{1,0:T(8,128)S(1)}, f32[160,256]{1,0:T(8,128)S(1)}, u32[]{:S(2)}, u32[]{:S(2)}) %collective-permute-start.2) | collective-permute-done | bytes 163872 | tf_op jit(solution)/shard_map/ppermute | solution.py:276
  77.7 1.7 collective-permute-done.8
  79.3 1.6 collective-permute-start.9
  80.9 2.1 %collective-permute-done.3 = f32[160,256]{1,0:T(8,128)S(1)} collective-permute-done((f32[160,256]{1,0:T(8,128)S(1)}, f32[160,256]{1,0:T(8,128)S(1)}, u32[]{:S(2)}, u32[]{:S(2)}) %collective-permute-start.3) | collective-permute-done | bytes 163872 | tf_op jit(solution)/shard_map/ppermute | solution.py:276
  83.1 1.6 collective-permute-start.4
  84.6 4.5 %collective-permute-done.9 = f32[320,256]{1,0:T(8,128)S(1)} collective-permute-done((f32[320,256]{1,0:T(8,128)S(1)}, f32[320,256]{1,0:T(8,128)S(1)}, u32[]{:S(2)}, u32[]{:S(2)}) %collective-permute-start.9) | collective-permute-done | bytes 327712 | tf_op jit(solution)/shard_map/ppermute | solution.py:276
  89.2 4.5 %collective-permute-done.4 = f32[320,256]{1,0:T(8,128)S(1)} collective-permute-done((f32[320,256]{1,0:T(8,128)S(1)}, f32[320,256]{1,0:T(8,128)S(1)}, u32[]{:S(2)}, u32[]{:S(2)}) %collective-permute-start.4) | collective-permute-done | bytes 327712 | tf_op jit(solution)/shard_map/ppermute | solution.py:276
  94.6 2.3 %right.3 = f32[896,256]{1,0:T(8,128)S(1)} custom-call(f32[1280,3456]{1,0:T(8,128)S(1)} %get-tuple-element.47.merged_ref, bf16[512,1280]{1,0:T(8,128)(2,1)S(1)} %get-tuple-element.48.turned_ref), custom_call_target="tpu_custom_call" | custom-call | flops 1761607680 | bytes 5872025 | tf_op jit(solution)/shard_map/right/pallas_call | solution.py:129
  96.9 3.3 %right.4 = f32[1536,256]{1,0:T(8,128)S(1)} custom-call(f32[1280,3456]{1,0:T(8,128)S(1)} %get-tuple-element.47.merged_ref, bf16[512,1280]{1,0:T(8,128)(2,1)S(1)} %get-tuple-element.48.turned_ref), custom_call_target="tpu_custom_call" | custom-call | flops 3019898880 | bytes 10066329 | tf_op jit(solution)/shard_map/right/pallas_call | solution.py:129
  101.0 2.3 %right.5 = f32[1024,256]{1,0:T(8,128)S(1)} custom-call(f32[1280,3456]{1,0:T(8,128)S(1)} %get-tuple-element.47.merged_ref, bf16[512,1280]{1,0:T(8,128)(2,1)S(1)} %get-tuple-element.48.turned_ref), custom_call_target="tpu_custom_call" | custom-call | flops 2013265920 | bytes 6710886 | tf_op jit(solution)/shard_map/right/pallas_call | solution.py:129
  104.1 1.6 collective-permute-start.14
  106.5 1.6 collective-permute-start.20
  108.7 38.9 %collective-permute-done.11 = f32[128,256]{1,0:T(8,128)S(1)} collective-permute-done((f32[128,256]{1,0:T(8,128)S(1)}, f32[128,256]{1,0:T(8,128)S(1)}, u32[]{:S(2)}, u32[]{:S(2)}) %collective-permute-start.11) | collective-permute-done | bytes 131104 | tf_op jit(solution)/shard_map/ppermute | solution.py:276
  147.6 1.3 collective-permute-done.12
  150.1 12.1 %ortho.1 = (f32[256,256]{1,0:T(8,128)S(1)}, f32[1280,256]{1,0:T(8,128)}, bf16[1280,768]{1,0:T(8,128)(2,1)S(1)}) custom-call(f32[256,256]{1,0:T(8,128)S(1)} %maximum_select_fusion.7.gram_ref, f32[1280,256]{1,0:T(8,128)S(1)} %pad_maximum_fusion.1.proj_ref), custom_call_target="tpu_custom_call" | custom-call | flops 40000000000 | bytes 133333336 | tf_op jit(solution)/shard_map/ortho/pallas_call | solution.py:205
  164.7 1.6 collective-permute-start.22
  166.2 4.0 %update.3.rest_0_ = f32[1280,3456]{1,0:T(8,128)} custom-call(bf16[1280,768]{1,0:T(8,128)(2,1)S(1)} %get-tuple-element.46.ortho_ref, f32[1280,3456]{1,0:T(8,128)S(1)} %get-tuple-element.47.merged_ref, f32[1024,256]{1,0:T(8,128)S(1)} %get-tuple-element.58.coeff_ref), custom_call_target="tpu_custom_call" | custom-call | flops 2013265920 | bytes 6710886 | tf_op jit(solution)/shard_map/update/pallas_call | solution.py:258
  170.2 1.7 collective-permute-start.23
  171.9 5.4 %update.4.rest_0_ = f32[1280,3456]{1,0:T(8,128)} custom-call(bf16[1280,768]{1,0:T(8,128)(2,1)S(1)} %get-tuple-element.46.ortho_ref, f32[1280,3456]{1,0:T(8,128)S(1)} %get-tuple-element.47.merged_ref, f32[1536,256]{1,0:T(8,128)S(1)} %get-tuple-element.55.coeff_ref, f32[1280,3456]{1,0:T(8,128)} %update.3.rest_0_), custom_call_target="tpu_custom_call", output_to_operand_aliasing={{}: (3, {})} | custom-call | flops 3019898880 | bytes 10066329 | tf_op jit(solution)/shard_map/update/pallas_call | solution.py:258
  177.4 3.7 %collective-permute-start.24 = (f32[1,256]{1,0:T(1,128)S(1)}, f32[1,256]{1,0:T(1,128)S(1)}, u32[]{:S(2)}, u32[]{:S(2)}) collective-permute-start(f32[1,256]{1,0:T(1,128)S(1)} %add.80), channel_id=1, source_target_pairs={{0,4},{1,5},{2,6},{3,7},{4,0},{5,1},{6,2},{7,3},{8,12},{9,13},{10,... | collective-permute-start | bytes 3080 | tf_op jit(solution)/shard_map/ppermute | solution.py:276
  181.1 3.8 %update.5 = f32[1280,3456]{1,0:T(8,128)} custom-call(bf16[1280,768]{1,0:T(8,128)(2,1)S(1)} %get-tuple-element.46.ortho_ref, f32[1280,3456]{1,0:T(8,128)S(1)} %get-tuple-element.47.merged_ref, f32[896,256]{1,0:T(8,128)S(1)} %get-tuple-element.52.coeff_ref, f32[1280,3456]{1,0:T(8,128)} %update.4.rest_0_), custom_call_target="tpu_custom_call", output_to_operand_aliasing={{}: (3, {})} | custom-call | flops 1761607680 | bytes 5872025 | tf_op jit(solution)/shard_map/update/pallas_call | solution.py:258
  185.1 2.0 %pad_maximum_fusion = f32[3456,256]{1,0:T(8,128)} fusion(f32[896,256]{1,0:T(8,128)S(1)} %broadcast_multiply_fusion.2, f32[1536,256]{1,0:T(8,128)S(1)} %broadcast_multiply_fusion, f32[1024,256]{1,0:T(8,128)S(1)} %broadcast_multiply_fusion.1), kind=kLoop, calls=%fused_computation | loop fusion | flops 1769472 | bytes 7077888 | tf_op jit(solution)/shard_map/concatenate | solution.py:353
  (71 shorter events, 11.3 us)
Async XLA Ops:
  40.4 18.9 %copy-start = (f32[640,256]{1,0:T(8,128)S(1)}, f32[640,256]{1,0:T(8,128)}, u32[]{:S(2)}) copy-start(f32[640,256]{1,0:T(8,128)} %get-tuple-element.37) | copy-start | bytes 1966084
  41.4 11.6 %collective-permute-start.5 = (f32[320,256]{1,0:T(8,128)S(1)}, f32[320,256]{1,0:T(8,128)S(1)}, u32[]{:S(2)}, u32[]{:S(2)}) collective-permute-start(f32[320,256]{1,0:T(8,128)S(1)} %constant_dynamic-slice_fusion.5), channel_id=1, source_target_pairs={{0,1},{1,0},{2,3},{3,2},{4,5},{5,4},{6,7},{7,6},{8,9},{9,8},{10,11... | collective-permute-start | bytes 983048 | tf_op jit(solution)/shard_map/ppermute | solution.py:276
  45.5 13.7 %collective-permute-start = (f32[320,256]{1,0:T(8,128)S(1)}, f32[320,256]{1,0:T(8,128)S(1)}, u32[]{:S(2)}, u32[]{:S(2)}) collective-permute-start(f32[320,256]{1,0:T(8,128)S(1)} %constant_dynamic-slice_fusion.7), channel_id=1, source_target_pairs={{0,1},{1,0},{2,3},{3,2},{4,5},{5,4},{6,7},{7,6},{8,9},{9,8},{10,11... | collective-permute-start | bytes 983048 | tf_op jit(solution)/shard_map/ppermute | solution.py:276
  54.1 7.1 %collective-permute-start.6 = (f32[160,256]{1,0:T(8,128)S(1)}, f32[160,256]{1,0:T(8,128)S(1)}, u32[]{:S(2)}, u32[]{:S(2)}) collective-permute-start(f32[160,256]{1,0:T(8,128)S(1)} %constant_dynamic-slice_fusion.4), channel_id=1, source_target_pairs={{0,2},{1,3},{2,0},{3,1},{4,6},{5,7},{6,4},{7,5},{8,10},{9,11},{10,... | collective-permute-start | bytes 491528 | tf_op jit(solution)/shard_map/ppermute | solution.py:276
  59.3 7.9 %collective-permute-start.1 = (f32[160,256]{1,0:T(8,128)S(1)}, f32[160,256]{1,0:T(8,128)S(1)}, u32[]{:S(2)}, u32[]{:S(2)}) collective-permute-start(f32[160,256]{1,0:T(8,128)S(1)} %constant_dynamic-slice_fusion.6), channel_id=1, source_target_pairs={{0,2},{1,3},{2,0},{3,1},{4,6},{5,7},{6,4},{7,5},{8,10},{9,11},{10,... | collective-permute-start | bytes 491528 | tf_op jit(solution)/shard_map/ppermute | solution.py:276
  61.2 12.7 %collective-permute-start.7 = (f32[160,256]{1,0:T(8,128)S(1)}, f32[160,256]{1,0:T(8,128)S(1)}, u32[]{:S(2)}, u32[]{:S(2)}) collective-permute-start(f32[160,256]{1,0:T(8,128)S(1)} %dynamic-slice_add_fusion.5), channel_id=1, source_target_pairs={{0,4},{1,5},{2,6},{3,7},{4,0},{5,1},{6,2},{7,3},{8,12},{9,13},{10,... | collective-permute-start | bytes 491528 | tf_op jit(solution)/shard_map/ppermute | solution.py:276
  67.2 10.3 %collective-permute-start.2 = (f32[160,256]{1,0:T(8,128)S(1)}, f32[160,256]{1,0:T(8,128)S(1)}, u32[]{:S(2)}, u32[]{:S(2)}) collective-permute-start(f32[160,256]{1,0:T(8,128)S(1)} %dynamic-slice_add_fusion.6), channel_id=1, source_target_pairs={{0,4},{1,5},{2,6},{3,7},{4,0},{5,1},{6,2},{7,3},{8,12},{9,13},{10,... | collective-permute-start | bytes 491528 | tf_op jit(solution)/shard_map/ppermute | solution.py:276
  73.9 5.4 %collective-permute-start.8 = (f32[160,256]{1,0:T(8,128)S(1)}, f32[160,256]{1,0:T(8,128)S(1)}, u32[]{:S(2)}, u32[]{:S(2)}) collective-permute-start(f32[160,256]{1,0:T(8,128)S(1)} %add.68), channel_id=1, source_target_pairs={{0,2},{1,3},{2,0},{3,1},{4,6},{5,7},{6,4},{7,5},{8,10},{9,11},{10,... | collective-permute-start | bytes 491528 | tf_op jit(solution)/shard_map/ppermute | solution.py:276
  77.6 5.5 %collective-permute-start.3 = (f32[160,256]{1,0:T(8,128)S(1)}, f32[160,256]{1,0:T(8,128)S(1)}, u32[]{:S(2)}, u32[]{:S(2)}) collective-permute-start(f32[160,256]{1,0:T(8,128)S(1)} %add.65), channel_id=1, source_target_pairs={{0,2},{1,3},{2,0},{3,1},{4,6},{5,7},{6,4},{7,5},{8,10},{9,11},{10,... | collective-permute-start | bytes 491528 | tf_op jit(solution)/shard_map/ppermute | solution.py:276
  79.3 9.8 %collective-permute-start.9 = (f32[320,256]{1,0:T(8,128)S(1)}, f32[320,256]{1,0:T(8,128)S(1)}, u32[]{:S(2)}, u32[]{:S(2)}) collective-permute-start(f32[320,256]{1,0:T(8,128)S(1)} %maximum_select_fusion.6), channel_id=1, source_target_pairs={{0,1},{1,0},{2,3},{3,2},{4,5},{5,4},{6,7},{7,6},{8,9},{9,8},{10,11... | collective-permute-start | bytes 983048 | tf_op jit(solution)/shard_map/ppermute | solution.py:276
  83.1 10.6 %collective-permute-start.4 = (f32[320,256]{1,0:T(8,128)S(1)}, f32[320,256]{1,0:T(8,128)S(1)}, u32[]{:S(2)}, u32[]{:S(2)}) collective-permute-start(f32[320,256]{1,0:T(8,128)S(1)} %maximum_select_fusion.5), channel_id=1, source_target_pairs={{0,1},{1,0},{2,3},{3,2},{4,5},{5,4},{6,7},{7,6},{8,9},{9,8},{10,11... | collective-permute-start | bytes 983048 | tf_op jit(solution)/shard_map/ppermute | solution.py:276
  100.3 5.4 %collective-permute-start.16 = (f32[768,256]{1,0:T(8,128)S(1)}, f32[768,256]{1,0:T(8,128)S(1)}, u32[]{:S(2)}, u32[]{:S(2)}) collective-permute-start(f32[768,256]{1,0:T(8,128)S(1)} %constant_dynamic-slice_fusion.1), channel_id=1, source_target_pairs={{0,8},{8,0},{16,24},{24,16},{1,9},{9,1},{17,25},{25,17},{2,10},{10... | collective-permute-start | bytes 2359304 | tf_op jit(solution)/shard_map/ppermute | solution.py:276
  100.5 3.6 %collective-permute-start.13 = (f32[448,256]{1,0:T(8,128)S(1)}, f32[448,256]{1,0:T(8,128)S(1)}, u32[]{:S(2)}, u32[]{:S(2)}) collective-permute-start(f32[448,256]{1,0:T(8,128)S(1)} %constant_dynamic-slice_fusion.2), channel_id=1, source_target_pairs={{0,8},{8,0},{16,24},{24,16},{1,9},{9,1},{17,25},{25,17},{2,10},{10... | collective-permute-start | bytes 1376264 | tf_op jit(solution)/shard_map/ppermute | solution.py:276
  103.4 3.0 %collective-permute-start.19 = (f32[512,256]{1,0:T(8,128)S(1)}, f32[512,256]{1,0:T(8,128)S(1)}, u32[]{:S(2)}, u32[]{:S(2)}) collective-permute-start(f32[512,256]{1,0:T(8,128)S(1)} %constant_dynamic-slice_fusion), channel_id=1, source_target_pairs={{0,8},{8,0},{16,24},{24,16},{1,9},{9,1},{17,25},{25,17},{2,10},{10... | collective-permute-start | bytes 1572872 | tf_op jit(solution)/shard_map/ppermute | solution.py:276
  103.5 4.5 %collective-permute-start.10 = (f32[128,256]{1,0:T(8,128)S(1)}, f32[128,256]{1,0:T(8,128)S(1)}, u32[]{:S(2)}, u32[]{:S(2)}) collective-permute-start(f32[128,256]{1,0:T(8,128)S(1)} %constant_dynamic-slice_fusion.3), channel_id=1, source_target_pairs={{0,8},{8,0},{16,24},{24,16},{1,9},{9,1},{17,25},{25,17},{2,10},{10... | collective-permute-start | bytes 393224 | tf_op jit(solution)/shard_map/ppermute | solution.py:276
  104.1 44.9 %collective-permute-start.14 = (f32[448,256]{1,0:T(8,128)S(1)}, f32[448,256]{1,0:T(8,128)S(1)}, u32[]{:S(2)}, u32[]{:S(2)}) collective-permute-start(f32[448,256]{1,0:T(8,128)S(1)} %dynamic-slice_add_fusion.2), channel_id=1, source_target_pairs={{0,16},{8,24},{16,0},{24,8},{1,17},{9,25},{17,1},{25,9},{2,18},{10... | collective-permute-start | bytes 1376264 | tf_op jit(solution)/shard_map/ppermute | solution.py:276
  105.8 44.0 %collective-permute-start.17 = (f32[768,256]{1,0:T(8,128)S(1)}, f32[768,256]{1,0:T(8,128)S(1)}, u32[]{:S(2)}, u32[]{:S(2)}) collective-permute-start(f32[768,256]{1,0:T(8,128)S(1)} %dynamic-slice_add_fusion), channel_id=1, source_target_pairs={{0,16},{8,24},{16,0},{24,8},{1,17},{9,25},{17,1},{25,9},{2,18},{10... | collective-permute-start | bytes 2359304 | tf_op jit(solution)/shard_map/ppermute | solution.py:276
  106.5 42.8 %collective-permute-start.20 = (f32[512,256]{1,0:T(8,128)S(1)}, f32[512,256]{1,0:T(8,128)S(1)}, u32[]{:S(2)}, u32[]{:S(2)}) collective-permute-start(f32[512,256]{1,0:T(8,128)S(1)} %dynamic-slice_add_fusion.1), channel_id=1, source_target_pairs={{0,16},{8,24},{16,0},{24,8},{1,17},{9,25},{17,1},{25,9},{2,18},{10... | collective-permute-start | bytes 1572872 | tf_op jit(solution)/shard_map/ppermute | solution.py:276
  108.1 39.5 %collective-permute-start.11 = (f32[128,256]{1,0:T(8,128)S(1)}, f32[128,256]{1,0:T(8,128)S(1)}, u32[]{:S(2)}, u32[]{:S(2)}) collective-permute-start(f32[128,256]{1,0:T(8,128)S(1)} %dynamic-slice_add_fusion.7), channel_id=1, source_target_pairs={{0,16},{8,24},{16,0},{24,8},{1,17},{9,25},{17,1},{25,9},{2,18},{10... | collective-permute-start | bytes 393224 | tf_op jit(solution)/shard_map/ppermute | solution.py:276
  147.6 1.4 collective-permute-start.12
  149.1 13.2 %collective-permute-start.15 = (f32[448,256]{1,0:T(8,128)S(1)}, f32[448,256]{1,0:T(8,128)S(1)}, u32[]{:S(2)}, u32[]{:S(2)}) collective-permute-start(f32[448,256]{1,0:T(8,128)S(1)} %add.72), channel_id=1, source_target_pairs={{0,8},{8,0},{16,24},{24,16},{1,9},{9,1},{17,25},{25,17},{2,10},{10... | collective-permute-start | bytes 1376264 | tf_op jit(solution)/shard_map/ppermute | solution.py:276
  149.4 13.5 %collective-permute-start.21 = (f32[512,256]{1,0:T(8,128)S(1)}, f32[512,256]{1,0:T(8,128)S(1)}, u32[]{:S(2)}, u32[]{:S(2)}) collective-permute-start(f32[512,256]{1,0:T(8,128)S(1)} %add.76), channel_id=1, source_target_pairs={{0,8},{8,0},{16,24},{24,16},{1,9},{9,1},{17,25},{25,17},{2,10},{10... | collective-permute-start | bytes 1572872 | tf_op jit(solution)/shard_map/ppermute | solution.py:276
  149.9 13.7 %collective-permute-start.18 = (f32[768,256]{1,0:T(8,128)S(1)}, f32[768,256]{1,0:T(8,128)S(1)}, u32[]{:S(2)}, u32[]{:S(2)}) collective-permute-start(f32[768,256]{1,0:T(8,128)S(1)} %add.74), channel_id=1, source_target_pairs={{0,8},{8,0},{16,24},{24,16},{1,9},{9,1},{17,25},{25,17},{2,10},{10... | collective-permute-start | bytes 2359304 | tf_op jit(solution)/shard_map/ppermute | solution.py:276
  164.7 5.6 %collective-permute-start.22 = (f32[1,256]{1,0:T(1,128)S(1)}, f32[1,256]{1,0:T(1,128)S(1)}, u32[]{:S(2)}, u32[]{:S(2)}) collective-permute-start(f32[1,256]{1,0:T(1,128)S(1)} %add_add_fusion), channel_id=1, source_target_pairs={{0,1},{1,0},{2,3},{3,2},{4,5},{5,4},{6,7},{7,6},{8,9},{9,8},{10,11... | collective-permute-start | bytes 3080 | tf_op jit(solution)/shard_map/ppermute | solution.py:276
  170.2 7.2 %collective-permute-start.23 = (f32[1,256]{1,0:T(1,128)S(1)}, f32[1,256]{1,0:T(1,128)S(1)}, u32[]{:S(2)}, u32[]{:S(2)}) collective-permute-start(f32[1,256]{1,0:T(1,128)S(1)} %add.79), channel_id=1, source_target_pairs={{0,2},{1,3},{2,0},{3,1},{4,6},{5,7},{6,4},{7,5},{8,10},{9,11},{10,... | collective-permute-start | bytes 3080 | tf_op jit(solution)/shard_map/ppermute | solution.py:276
  177.4 7.5 %collective-permute-start.24 = (f32[1,256]{1,0:T(1,128)S(1)}, f32[1,256]{1,0:T(1,128)S(1)}, u32[]{:S(2)}, u32[]{:S(2)}) collective-permute-start(f32[1,256]{1,0:T(1,128)S(1)} %add.80), channel_id=1, source_target_pairs={{0,4},{1,5},{2,6},{3,7},{4,0},{5,1},{6,2},{7,3},{8,12},{9,13},{10,... | collective-permute-start | bytes 3080 | tf_op jit(solution)/shard_map/ppermute | solution.py:276
